TPU v7x, 512 devices: a whole 4x4x16 slice. The times are simulated.
512 devices in a mesh: dp: 32 (over z, core), tp: 16 (over x, y).
Axes of the slice: x: 4, y: 4, z: 16, core: 2. Of those that a mesh axis runs over, the one named last changes fastest.
Arguments:
- partials: bfloat16 [16, 5120, 7680], P('tp', 'dp'), may hold values from -1.5 to 1.5
- layer_input: bfloat16 [7680, 1280], P(('dp', 'tp')), may hold values from -6 to 6
- ln_gain: float32 [1280], replicated, may hold values from 0.25 to 1.75
- ln_bias: float32 [1280], replicated, may hold values from -3 to 3
- fc1_weight: bfloat16 [1280, 5120], P(None, 'tp'), may hold values from -0.15625 to 0.15625
- fc1_bias: float32 [5120], P('tp'), may hold values from -3 to 3
- fc2_weight: bfloat16 [1280, 5120], P(None, 'tp'), may hold values from -0.078125 to 0.078125
- row_rank: int32 [5120, 1], P('dp'), may hold values from 0 to 15; in each aligned block of 160 rows (0 to 159, 160 to 319, ...) at most 15 rows name the same one
Outputs:
- early_grads: bfloat16 [7680, 6400], P(('dp', 'tp'))
- fc1_grad: bfloat16 [1280, 5120], P('dp', 'tp')
- fc2_grad: bfloat16 [1280, 5120], P('dp', 'tp')
Inputs may be any that keep to these rules, and one draw needn't show every extreme that they name: `row_rank`: in each aligned block of 160 rows (one data replica) no rank is named by more than 15 rows, a bound that some block reaches.
All inputs are finite; a program needn't handle non-finite values.
Results may differ from a plain program's by a relative error of at most 0.029.
Values may be sent and summed in bfloat16 or wider, within the bound.
No kernel may reach another device: no remote copies, remote signals or barrier semaphores. Data moves between devices by JAX's collectives and lax.ppermute only.
A program may use at most 64 MiB of HBM per device.

v0:
```python
import functools

import jax
import jax.numpy as jnp
from jax import lax
from jax.experimental import pallas as pl
from jax.experimental.pallas import tpu as pltpu
from jax.sharding import PartitionSpec as P


SUB, LANE = 8, 128
SLOT_PAD = 16


def tile_places(rows, width, parts):
    across = width // LANE
    total = (rows // SUB) * across
    whole = total // parts
    places = []
    for t in range(total):
        r, c = divmod(t, across)
        if t < whole * parts:
            places.append((*divmod(t, whole), 0, SUB, r * SUB, c * LANE))
        else:
            half = SUB // 2
            for h in range(2):
                part = 2 * (t - whole * parts) + h
                places.append((part, whole, 0, half, r * SUB + h * half, c * LANE))
    return whole + 1, places


def cut_kernel(places, x_ref, layer_ref, out_ref):
    parts, depth = out_ref.shape[:2]
    slot_count, width = layer_ref.shape
    across = width // LANE
    head = depth - (SLOT_PAD // SUB) * across
    for part, i, at, size, r, c in places:
        out_ref[part, i, at : at + size, :] = x_ref[r : r + size, c : c + LANE]
        if size < SUB:
            out_ref[part, i, size:, :] = jnp.zeros((SUB - size, LANE), out_ref.dtype)
    for at in range(0, SLOT_PAD, SUB):
        size = min(SUB, slot_count - at)
        for c in range(across):
            tile = layer_ref[at : at + size, c * LANE : (c + 1) * LANE]
            for part in range(parts):
                out_ref[part, head + (at // SUB) * across + c, :size, :] = tile
                if size < SUB:
                    out_ref[part, head + (at // SUB) * across + c, size:, :] = jnp.zeros((SUB - size, LANE), tile.dtype)


def cut_tiles(x, layer, parts):
    rows, width = x.shape[0], layer.shape[1]
    depth, places = tile_places(rows, width, parts)
    depth += (SLOT_PAD // SUB) * (width // LANE)
    return pl.pallas_call(
        functools.partial(cut_kernel, places),
        grid=(1,),
        in_specs=[pl.BlockSpec((rows, width), lambda i: (0, 0)), pl.BlockSpec(layer.shape, lambda i: (0, 0))],
        out_specs=pl.BlockSpec((parts, depth, SUB, LANE), lambda i: (0, 0, 0, 0)),
        out_shape=jax.ShapeDtypeStruct((parts, depth, SUB, LANE), x.dtype),
        name="cut_tiles",
    )(x, layer)


def gelu_parts(preact):
    normal_cdf = 0.5 * (1.0 + lax.erf(preact * 0.7071067811865476))
    density = jnp.exp(-0.5 * preact * preact) * 0.3989422804014327
    return (preact * normal_cdf, normal_cdf + preact * density)


def hidden_kernel(head, tiles_ref, gain_ref, bias_ref, weight_ref, fc1_bias_ref, normed_ref, hidden_ref, deriv_ref):
    parts = tiles_ref.shape[0]
    slots, width = normed_ref.shape
    across = width // LANE
    per_part = slots // parts
    for part in range(parts):
        for at in range(0, per_part, SUB):
            for c in range(across):
                normed_ref[part * per_part + at : part * per_part + at + SUB, c * LANE : (c + 1) * LANE] = tiles_ref[
                    part, head + (at // SUB) * across + c
                ]
    values = normed_ref[...].astype(jnp.float32)
    centered = values - jnp.mean(values, axis=1, keepdims=True)
    row_var = jnp.mean(centered * centered, axis=1, keepdims=True)
    normed = (centered / jnp.sqrt(row_var + 1e-05) * gain_ref[...][None] + bias_ref[...][None]).astype(jnp.bfloat16)
    normed_ref[...] = normed
    preact = lax.dot_general(normed, weight_ref[...], (((1,), (1,)), ((), ())), preferred_element_type=jnp.float32)
    activated, derivative = gelu_parts(preact + fc1_bias_ref[...][None])
    gap = hidden_ref.shape[1] - activated.shape[1]
    hidden_ref[...] = jnp.zeros_like(hidden_ref)
    hidden_ref[:, gap:] = activated.astype(jnp.bfloat16)
    deriv_ref[...] = derivative


def hidden_parts(tiles, head, gain, bias, weight_t, fc1_bias):
    units, width = weight_t.shape
    slots = tiles.shape[0] * SLOT_PAD
    wide = -(-units // LANE) * LANE
    return pl.pallas_call(
        functools.partial(hidden_kernel, head),
        out_shape=(
            jax.ShapeDtypeStruct((slots, width), jnp.bfloat16),
            jax.ShapeDtypeStruct((slots, wide), jnp.bfloat16),
            jax.ShapeDtypeStruct((slots, units), jnp.float32),
        ),
        name="hidden_parts",
    )(tiles, gain, bias, weight_t, fc1_bias)


def grads_kernel(places, factor, tiles_ref, table_ref, normed_ref, hidden_ref, deriv_ref, weight_ref, mine_ref, theirs_ref, rows_ref, up_ref, pg_ref):
    for part, i, at, size, r, c in places:
        rows_ref[r : r + size, c : c + LANE] = tiles_ref[part, i, at : at + size, :]
    up_ref[...] = jnp.dot(table_ref[...], rows_ref[...], preferred_element_type=jnp.float32).astype(jnp.bfloat16)
    hidden_grad = lax.dot_general(
        up_ref[...], weight_ref[...], (((1,), (1,)), ((), ())), preferred_element_type=jnp.float32
    )
    units = hidden_grad.shape[1]
    pg_ref[...] = jnp.zeros_like(pg_ref)
    pg_ref[:, :units] = (hidden_grad * deriv_ref[...]).astype(jnp.bfloat16)
    near, _, block, _ = mine_ref.shape
    wide = pg_ref.shape[1]
    keep = wide - LANE
    step = 5 * LANE
    low = lax.axis_index("dp") % 2 == 0
    for at in range(0, normed_ref.shape[1], step):
        dims = (((0,), (0,)), ((), ()))
        first = lax.dot_general(normed_ref[:, at : at + step], pg_ref[...], dims, preferred_element_type=jnp.float32)
        second = lax.dot_general(up_ref[:, at : at + step], hidden_ref[...], dims, preferred_element_type=jnp.float32)
        for b in range(0, step, 2 * block):
            m, p = divmod((at + b) // (2 * block), near)
            parts = []
            for half in (b, b + block):
                one, two = first[half : half + block] * factor, second[half : half + block] * factor
                parts.append((one[:, :keep], one[:, keep:] + two[:, :LANE], two[:, LANE:]))
            for lo, hi, start in zip(*parts, (0, keep, wide)):
                mine_ref[p, m, :, start : start + lo.shape[1]] = jnp.where(low, lo, hi).astype(jnp.bfloat16)
                theirs_ref[p, m, :, start : start + lo.shape[1]] = jnp.where(low, hi, lo).astype(jnp.bfloat16)


def grad_terms(tiles, table, normed, hidden, deriv, weight_t, factor, shape):
    slots, width = normed.shape
    rows = table.shape[1]
    _, places = tile_places(rows, width, tiles.shape[0])
    return pl.pallas_call(
        functools.partial(grads_kernel, places, factor),
        out_shape=(jax.ShapeDtypeStruct(shape, jnp.bfloat16),) * 2,
        scratch_shapes=[
            pltpu.VMEM((rows, width), jnp.bfloat16),
            pltpu.VMEM((slots, width), jnp.bfloat16),
            pltpu.VMEM((slots, hidden.shape[1]), jnp.bfloat16),
        ],
        name="grad_terms",
    )(tiles, table, normed, hidden, deriv, weight_t)


def tables_kernel(side, ranks_ref, table_ref, early_ref):
    rows = ranks_ref.shape[1]
    slots = table_ref.shape[0]
    groups = slots // SLOT_PAD
    ranks = ranks_ref[...]
    hot = lax.broadcasted_iota(jnp.int32, (groups, rows), 0) == ranks
    earlier = lax.broadcasted_iota(jnp.int32, (rows, rows), 0) < lax.broadcasted_iota(jnp.int32, (rows, rows), 1)
    before = jnp.dot(
        hot.astype(jnp.float32).astype(jnp.bfloat16),
        earlier.astype(jnp.float32).astype(jnp.bfloat16),
        preferred_element_type=jnp.float32,
    )
    position = jnp.sum(jnp.where(hot, before, 0.0), axis=0, keepdims=True).astype(jnp.int32)
    targets = lax.broadcasted_iota(jnp.int32, (slots, rows), 0)
    table_ref[...] = (targets == ranks * SLOT_PAD + position).astype(jnp.float32).astype(jnp.bfloat16)
    shift = side.bit_length() - 1
    me = lax.axis_index("tp")
    dx = ((ranks >> shift) - (me >> shift)) & (side - 1)
    dy = ((ranks & (side - 1)) - (me & (side - 1))) & (side - 1)
    x_first = lax.axis_index("dp") % 2 == 0
    where_to = jnp.where(x_first, dx * side + dy, dy * side + dx)
    early_ref[...] = (targets == where_to * SLOT_PAD + position).astype(jnp.float32).astype(jnp.bfloat16)


def slot_tables(rank_ids, groups):
    shape = jax.ShapeDtypeStruct((groups * SLOT_PAD, rank_ids.shape[1]), jnp.bfloat16)
    return pl.pallas_call(
        functools.partial(tables_kernel, int(groups**0.5)), out_shape=(shape, shape), name="slot_tables",
    )(rank_ids)


def exchange(blocks, axis, groups=None):
    return lax.all_to_all(blocks, axis, 0, 0, tiled=True, axis_index_groups=groups)


def to_all(shard, axis):
    return exchange(jnp.broadcast_to(shard, (lax.axis_size(axis), *shard.shape)), axis)


def total(arrived):
    return arrived.astype(jnp.float32).sum(axis=0).astype(jnp.bfloat16)


def plane_rounds(replicas, side):
    rounds = []
    for turn in range(2):
        perms = []
        for d in range(1, side):
            pairs = []
            for k in range(replicas):
                for x in range(side):
                    for y in range(side):
                        along_x = (k % 2 == 0) == (turn == 0)
                        to = ((x + d) % side, y) if along_x else (x, (y + d) % side)
                        pairs.append(((k * side + x) * side + y, (k * side + to[0]) * side + to[1]))
            perms.append(pairs)
        rounds.append(perms)
    return rounds


def named_permute(value, pairs):
    return lax.ppermute(value, ("dp", "tp"), pairs)


def summed(own, moved):
    return sum((b.astype(jnp.float32) for b in moved), own.astype(jnp.float32)).astype(jnp.bfloat16)


def route_early(part, table, replicas, groups):
    side = int(groups**0.5)
    rounds = plane_rounds(replicas, side)
    span = side * SLOT_PAD
    blocks = []
    for d in range(side):
        block = jnp.dot(table[d * span : (d + 1) * span], part, preferred_element_type=jnp.float32)
        blocks.append(block.astype(jnp.bfloat16))
    moved = [named_permute(blocks[d], rounds[0][d - 1]) for d in range(1, side)]
    half_way = summed(lax.optimization_barrier(blocks[0]), moved)
    pieces = [half_way[d * SLOT_PAD : (d + 1) * SLOT_PAD] for d in range(side)]
    moved = [named_permute(pieces[d], rounds[1][d - 1]) for d in range(1, side)]
    return summed(pieces[0], moved)


def dp_groups(replicas):
    cores, near = 2, 4
    depth = replicas // cores
    far = depth // near
    pairs = [(k, k ^ 1) for k in range(replicas)]
    close = []
    for g in range(far):
        close.append([cores * (near * g + p) for p in range(near)])
    for g in range(far):
        zs = [(near * (g + 1) + p) % depth if p < near // 2 else near * g + p for p in range(near)]
        close.append([cores * z + 1 for z in zs])
    strided = [[cores * (near * m + p) + c for m in range(far)] for p in range(near) for c in range(cores)]
    return cores, near, far, pairs, close, strided


def shards(partials, layer_input, ln_gain, ln_bias, fc1_weight, fc1_bias, fc2_weight, row_rank):
    groups = lax.axis_size("tp")
    replicas = lax.axis_size("dp")
    local_part = partials[0]
    row_count = local_part.shape[0]
    slot_count, width = layer_input.shape
    units = fc1_weight.shape[1]
    _, near, far, pairs, close, strided = dp_groups(replicas)
    block = width // replicas

    arrived = exchange(cut_tiles(local_part, layer_input, groups), "tp")
    head = arrived.shape[1] - (SLOT_PAD // SUB) * (width // LANE)
    own_tiles = total(arrived[:, :head])
    tiles = to_all(own_tiles, "tp")

    table, early_table = slot_tables(row_rank.T, groups)
    normed_all, hidden, derivative = hidden_parts(arrived, head, ln_gain, ln_bias, fc1_weight.T, fc1_bias)
    placed = route_early(local_part[:, width:], early_table, replicas, groups)[:slot_count]

    factor = float(replicas * row_count) ** (-0.5)
    mine, theirs = grad_terms(
        tiles, table, normed_all, hidden, derivative, fc2_weight.T, factor,
        (near, far, block, 2 * units),
    )
    theirs = lax.ppermute(theirs, "dp", pairs)
    both = summed(mine, (theirs,))
    both = exchange(both, "dp", close)
    both = total(both)
    both = exchange(both, "dp", strided)
    both = total(both)
    return (placed, both[:, :units], both[:, units:])


def solution(mesh):
    return jax.shard_map(
        shards,
        mesh=mesh,
        in_specs=(
            P("tp", "dp", None),
            P(("dp", "tp"), None),
            P(),
            P(),
            P(None, "tp"),
            P("tp"),
            P(None, "tp"),
            P("dp", None),
        ),
        out_specs=(P(("dp", "tp"), None), P("dp", "tp"), P("dp", "tp")),
        check_vma=False,
    )
```

profile of v0, /device:TPU:56, one launch (start us, length us, event | category | flops | bytes accessed | tf_op | source)
XLA Modules:
  0.0 117.4 jit_solution(1890860825460971958)
XLA Ops:
  0.6 2.2 %cut_tiles.1 = bf16[16,33,8,128]{3,2,1,0:T(8,128)(2,1)} custom-call(bf16[160,7680]{1,0:T(8,128)(2,1)} %bitcast.4, bf16[15,1280]{1,0:T(8,128)(2,1)} %layer_ref.1), custom_call_target="tpu_custom_call" | custom-call | tf_op jit(solution)/shard_map/cut_tiles/pallas_call | solution.py:55
  2.8 7.3 %all-to-all-start = ((bf16[16,33,8,128]{3,2,1,0:T(8,128)(2,1)}), bf16[16,33,8,128]{3,2,1,0:T(8,128)(2,1)S(1)}, u32[]{:S(2)}, u32[]{:S(2)}) async-start(bf16[16,33,8,128]{3,2,1,0:T(8,128)(2,1)} %cut_tiles.1), calls=%async_computation | async-start | bytes 2162688 | tf_op jit(solution)/shard_map/all_to_all | solution.py:188
  10.1 1.6 %slot_tables.1 = (bf16[256,160]{1,0:T(8,128)(2,1)}, bf16[256,160]{1,0:T(8,128)(2,1)}) custom-call(s32[1,160]{1,0:T(1,128)} %bitcast.11), custom_call_target="tpu_custom_call" | custom-call | tf_op jit(solution)/shard_map/slot_tables/pallas_call | solution.py:182
  11.7 13.6 %all-to-all-done.tiles_ref = bf16[16,33,8,128]{3,2,1,0:T(8,128)(2,1)S(1)} async-done(((bf16[16,33,8,128]{3,2,1,0:T(8,128)(2,1)}), bf16[16,33,8,128]{3,2,1,0:T(8,128)(2,1)S(1)}, u32[]{:S(2)}, u32[]{:S(2)}) %all-to-all-start) | async-done | bytes 1081376 | tf_op jit(solution)/shard_map/all_to_all | solution.py:188
  25.3 0.1 slice_reduce_fusion
  25.4 0.9 broadcast_in_dim.3
  26.3 7.1 %all-to-all-start.1 = ((bf16[16,13,8,128]{3,2,1,0:T(8,128)(2,1)}), bf16[16,13,8,128]{3,2,1,0:T(8,128)(2,1)}, u32[]{:S(2)}, u32[]{:S(2)}) async-start(bf16[16,13,8,128]{3,2,1,0:T(8,128)(2,1)} %broadcast_in_dim.3), calls=%async_computation.1 | async-start | bytes 851968 | tf_op jit(solution)/shard_map/all_to_all | solution.py:188
  33.4 2.1 %convolution_convert_fusion.2 = bf16[64,6400]{1,0:T(8,128)(2,1)} fusion(bf16[160,7680]{1,0:T(8,128)(2,1)S(1)} %bitcast.5, bf16[256,160]{1,0:T(8,128)(2,1)} %get-tuple-element.10), kind=kOutput, calls=%fused_computation.2 | convolution fusion | flops 131481600 | bytes 2899968 | tf_op jit(solution)/shard_map/dot_general | solution.py:230
  35.5 3.4 %collective-permute-start = (bf16[64,6400]{1,0:T(8,128)(2,1)}, bf16[64,6400]{1,0:T(8,128)(2,1)}, u32[]{:S(2)}, u32[]{:S(2)}) collective-permute-start(bf16[64,6400]{1,0:T(8,128)(2,1)} %convolution_convert_fusion.2), channel_id=1, source_target_pairs={{0,4},{1,5},{2,6},{3,7},{4,8},{5,9},{6,10},{7,11},{8,12},{9,13},{1... | collective-permute-start | bytes 2457608 | tf_op jit(solution)/shard_map/ppermute | solution.py:217
  38.8 2.1 %convolution_convert_fusion.1 = bf16[64,6400]{1,0:T(8,128)(2,1)} fusion(bf16[160,7680]{1,0:T(8,128)(2,1)S(1)} %bitcast.6, bf16[256,160]{1,0:T(8,128)(2,1)} %get-tuple-element.10), kind=kOutput, calls=%fused_computation.1 | convolution fusion | flops 131481600 | bytes 2899968 | tf_op jit(solution)/shard_map/dot_general | solution.py:230
  40.9 4.7 %collective-permute-start.1 = (bf16[64,6400]{1,0:T(8,128)(2,1)}, bf16[64,6400]{1,0:T(8,128)(2,1)}, u32[]{:S(2)}, u32[]{:S(2)}) collective-permute-start(bf16[64,6400]{1,0:T(8,128)(2,1)} %convolution_convert_fusion.1), channel_id=1, source_target_pairs={{0,8},{1,9},{2,10},{3,11},{4,12},{5,13},{6,14},{7,15},{8,0},{9,1},... | collective-permute-start | bytes 2457608 | tf_op jit(solution)/shard_map/ppermute | solution.py:217
  45.6 3.4 %hidden_parts.1 = (bf16[256,1280]{1,0:T(8,128)(2,1)}, bf16[256,384]{1,0:T(8,128)(2,1)}, f32[256,320]{1,0:T(8,128)}) custom-call(bf16[16,33,8,128]{3,2,1,0:T(8,128)(2,1)} %copy-done.1, f32[1280]{0:T(1024)} %gain_ref.1, f32[1280]{0:T(1024)} %bias_ref.1, bf16[320,1280]{1,0:T(8,128)(2,1)} %bitcast.9, f32[320]{0:T(512)} %fc1_bias_ref.1), custom_call_target="tpu_custom_call" | custom-call | tf_op jit(solution)/shard_map/hidden_parts/pallas_call | solution.py:99
  49.0 4.5 %grad_terms.1 = (bf16[4,4,40,640]{3,2,1,0:T(8,128)(2,1)}, bf16[4,4,40,640]{3,2,1,0:T(8,128)(2,1)}) custom-call(bf16[16,13,8,128]{3,2,1,0:T(8,128)(2,1)} %all-to-all-done.1.tiles_ref, bf16[256,160]{1,0:T(8,128)(2,1)} %get-tuple-element.11.table_ref, bf16[256,1280]{1,0:T(8,128)(2,1)} %get-tuple-element.12.normed_ref, ...), custom_call_target="tpu_custom_call" | custom-call | tf_op jit(solution)/shard_map/grad_terms/pallas_call | solution.py:144
  53.6 1.9 %collective-permute-start.6 = (bf16[4,4,40,640]{3,2,1,0:T(8,128)(2,1)}, bf16[4,4,40,640]{3,2,1,0:T(8,128)(2,1)S(1)}, u32[]{:S(2)}, u32[]{:S(2)}) collective-permute-start(bf16[4,4,40,640]{3,2,1,0:T(8,128)(2,1)} %get-tuple-element.16), channel_id=1, source_target_pairs={{0,16},{16,0},{32,48},{48,32},{64,80},{80,64},{96,112},{112,96},{1... | collective-permute-start | bytes 2457608 | tf_op jit(solution)/shard_map/ppermute | solution.py:278
  55.5 1.3 %convolution_convert_fusion = bf16[64,6400]{1,0:T(8,128)(2,1)} fusion(bf16[160,7680]{1,0:T(8,128)(2,1)S(1)} %bitcast.7, bf16[256,160]{1,0:T(8,128)(2,1)S(1)} %copy-done.3), kind=kOutput, calls=%fused_computation | convolution fusion | flops 131481600 | bytes 2899968 | tf_op jit(solution)/shard_map/dot_general | solution.py:230
  56.8 3.4 %collective-permute-start.2 = (bf16[64,6400]{1,0:T(8,128)(2,1)}, bf16[64,6400]{1,0:T(8,128)(2,1)}, u32[]{:S(2)}, u32[]{:S(2)}) collective-permute-start(bf16[64,6400]{1,0:T(8,128)(2,1)} %convolution_convert_fusion), channel_id=1, source_target_pairs={{0,12},{1,13},{2,14},{3,15},{4,0},{5,1},{6,2},{7,3},{8,4},{9,5},{1... | collective-permute-start | bytes 2457608 | tf_op jit(solution)/shard_map/ppermute | solution.py:217
  60.3 0.4 convolution_convert_fusion.3
  60.7 1.1 add_convert_fusion
  61.8 6.0 %all-to-all-start.2 = ((bf16[4,4,40,640]{3,2,1,0:T(8,128)(2,1)}), bf16[4,4,40,640]{3,2,1,0:T(8,128)(2,1)S(1)}, u32[]{:S(2)}, u32[]{:S(2)}) async-start(bf16[4,4,40,640]{3,2,1,0:T(8,128)(2,1)} %add_convert_fusion), calls=%async_computation.2 | async-start | bytes 1638400 | tf_op jit(solution)/shard_map/all_to_all | solution.py:188
  67.8 0.0 collective-permute-done
  67.9 3.6 %collective-permute-done.2 = bf16[64,6400]{1,0:T(8,128)(2,1)} collective-permute-done((bf16[64,6400]{1,0:T(8,128)(2,1)}, bf16[64,6400]{1,0:T(8,128)(2,1)}, u32[]{:S(2)}, u32[]{:S(2)}) %collective-permute-start.2) | collective-permute-done | bytes 819232 | tf_op jit(solution)/shard_map/ppermute | solution.py:217
  71.5 2.0 %add_convert_fusion.1 = bf16[64,6400]{1,0:T(8,128)(2,1)S(1)} fusion(bf16[64,6400]{1,0:T(8,128)(2,1)} %collective-permute-done.2, bf16[64,6400]{1,0:T(8,128)(2,1)} %collective-permute-done.1, bf16[64,6400]{1,0:T(8,128)(2,1)} %collective-permute-done, bf16[64,6400]{1,0:T(8,128)(2,1)S(1)} %convolution_convert_fusion.3), kind=kLoop, calls=%fused_computation.5 | loop fusion | flops 3276800 | bytes 4096000 | tf_op jit(solution)/shard_map/convert_element_type | solution.py:221
  73.5 0.1 fusion.8
  73.6 2.4 %collective-permute-start.3 = (bf16[16,6400]{1,0:T(8,128)(2,1)S(1)}, bf16[16,6400]{1,0:T(8,128)(2,1)S(1)}, u32[]{:S(2)}, u32[]{:S(2)}) collective-permute-start(bf16[16,6400]{1,0:T(8,128)(2,1)S(1)} %get-tuple-element.20), channel_id=1, source_target_pairs={{0,1},{1,2},{2,3},{3,0},{4,5},{5,6},{6,7},{7,4},{8,9},{9,10},{10,1... | collective-permute-start | bytes 614408 | tf_op jit(solution)/shard_map/ppermute | solution.py:217
  76.0 4.3 %collective-permute-start.4 = (bf16[16,6400]{1,0:T(8,128)(2,1)S(1)}, bf16[16,6400]{1,0:T(8,128)(2,1)S(1)}, u32[]{:S(2)}, u32[]{:S(2)}) collective-permute-start(bf16[16,6400]{1,0:T(8,128)(2,1)S(1)} %get-tuple-element.19), channel_id=1, source_target_pairs={{0,2},{1,3},{2,0},{3,1},{4,6},{5,7},{6,4},{7,5},{8,10},{9,11},{10,... | collective-permute-start | bytes 614408 | tf_op jit(solution)/shard_map/ppermute | solution.py:217
  80.3 1.9 %collective-permute-start.5 = (bf16[16,6400]{1,0:T(8,128)(2,1)S(1)}, bf16[16,6400]{1,0:T(8,128)(2,1)S(1)}, u32[]{:S(2)}, u32[]{:S(2)}) collective-permute-start(bf16[16,6400]{1,0:T(8,128)(2,1)S(1)} %get-tuple-element.18), channel_id=1, source_target_pairs={{0,3},{1,0},{2,1},{3,2},{4,7},{5,4},{6,5},{7,6},{8,11},{9,8},{10,9... | collective-permute-start | bytes 614408 | tf_op jit(solution)/shard_map/ppermute | solution.py:217
  82.2 2.9 %all-to-all-done.2 = bf16[4,4,40,640]{3,2,1,0:T(8,128)(2,1)S(1)} async-done(((bf16[4,4,40,640]{3,2,1,0:T(8,128)(2,1)}), bf16[4,4,40,640]{3,2,1,0:T(8,128)(2,1)S(1)}, u32[]{:S(2)}, u32[]{:S(2)}) %all-to-all-start.2) | async-done | bytes 819232 | tf_op jit(solution)/shard_map/all_to_all | solution.py:188
  85.1 0.8 reduce_sum.37
  86.0 11.3 %all-to-all-start.3 = ((bf16[4,40,640]{2,1,0:T(8,128)(2,1)}), bf16[4,40,640]{2,1,0:T(8,128)(2,1)S(1)}, u32[]{:S(2)}, u32[]{:S(2)}) async-start(bf16[4,40,640]{2,1,0:T(8,128)(2,1)} %reduce_sum.37), calls=%async_computation.3 | async-start | bytes 409600 | tf_op jit(solution)/shard_map/all_to_all | solution.py:188
  97.3 0.8 add_convert_fusion.2
  98.1 18.6 %all-to-all-done.3 = bf16[4,40,640]{2,1,0:T(8,128)(2,1)S(1)} async-done(((bf16[4,40,640]{2,1,0:T(8,128)(2,1)}), bf16[4,40,640]{2,1,0:T(8,128)(2,1)S(1)}, u32[]{:S(2)}, u32[]{:S(2)}) %all-to-all-start.3) | async-done | bytes 204832 | tf_op jit(solution)/shard_map/all_to_all | solution.py:188
  116.7 0.7 fusion.9
  (15 shorter events, 0.1 us)
Async XLA Ops:
  2.8 30.5 %copy-start = (bf16[1,160,7680]{2,1,0:T(8,128)(2,1)S(1)}, bf16[1,160,7680]{2,1,0:T(8,128)(2,1)}, u32[]{:S(2)}) copy-start(bf16[1,160,7680]{2,1,0:T(8,128)(2,1)} %param.8) | copy-start | bytes 7372804
  2.8 22.5 %all-to-all-start = ((bf16[16,33,8,128]{3,2,1,0:T(8,128)(2,1)}), bf16[16,33,8,128]{3,2,1,0:T(8,128)(2,1)S(1)}, u32[]{:S(2)}, u32[]{:S(2)}) async-start(bf16[16,33,8,128]{3,2,1,0:T(8,128)(2,1)} %cut_tiles.1), calls=%async_computation | async-start | bytes 2162688 | tf_op jit(solution)/shard_map/all_to_all | solution.py:188
  25.3 10.2 %copy-start.1 = (bf16[16,33,8,128]{3,2,1,0:T(8,128)(2,1)}, bf16[16,33,8,128]{3,2,1,0:T(8,128)(2,1)S(1)}, u32[]{:S(2)}) copy-start(bf16[16,33,8,128]{3,2,1,0:T(8,128)(2,1)S(1)} %all-to-all-done.tiles_ref) | copy-start | bytes 3244036
  26.3 22.7 %all-to-all-start.1 = ((bf16[16,13,8,128]{3,2,1,0:T(8,128)(2,1)}), bf16[16,13,8,128]{3,2,1,0:T(8,128)(2,1)}, u32[]{:S(2)}, u32[]{:S(2)}) async-start(bf16[16,13,8,128]{3,2,1,0:T(8,128)(2,1)} %broadcast_in_dim.3), calls=%async_computation.1 | async-start | bytes 851968 | tf_op jit(solution)/shard_map/all_to_all | solution.py:188
  35.5 32.4 %collective-permute-start = (bf16[64,6400]{1,0:T(8,128)(2,1)}, bf16[64,6400]{1,0:T(8,128)(2,1)}, u32[]{:S(2)}, u32[]{:S(2)}) collective-permute-start(bf16[64,6400]{1,0:T(8,128)(2,1)} %convolution_convert_fusion.2), channel_id=1, source_target_pairs={{0,4},{1,5},{2,6},{3,7},{4,8},{5,9},{6,10},{7,11},{8,12},{9,13},{1... | collective-permute-start | bytes 2457608 | tf_op jit(solution)/shard_map/ppermute | solution.py:217
  40.9 26.9 %collective-permute-start.1 = (bf16[64,6400]{1,0:T(8,128)(2,1)}, bf16[64,6400]{1,0:T(8,128)(2,1)}, u32[]{:S(2)}, u32[]{:S(2)}) collective-permute-start(bf16[64,6400]{1,0:T(8,128)(2,1)} %convolution_convert_fusion.1), channel_id=1, source_target_pairs={{0,8},{1,9},{2,10},{3,11},{4,12},{5,13},{6,14},{7,15},{8,0},{9,1},... | collective-permute-start | bytes 2457608 | tf_op jit(solution)/shard_map/ppermute | solution.py:217
  45.6 9.9 %copy-start.3 = (bf16[256,160]{1,0:T(8,128)(2,1)S(1)}, bf16[256,160]{1,0:T(8,128)(2,1)}, u32[]{:S(2)}) copy-start(bf16[256,160]{1,0:T(8,128)(2,1)} %get-tuple-element.10) | copy-start | bytes 245764
  53.6 7.1 %collective-permute-start.6 = (bf16[4,4,40,640]{3,2,1,0:T(8,128)(2,1)}, bf16[4,4,40,640]{3,2,1,0:T(8,128)(2,1)S(1)}, u32[]{:S(2)}, u32[]{:S(2)}) collective-permute-start(bf16[4,4,40,640]{3,2,1,0:T(8,128)(2,1)} %get-tuple-element.16), channel_id=1, source_target_pairs={{0,16},{16,0},{32,48},{48,32},{64,80},{80,64},{96,112},{112,96},{1... | collective-permute-start | bytes 2457608 | tf_op jit(solution)/shard_map/ppermute | solution.py:278
  56.8 3.9 %copy-start.2 = (bf16[4,4,40,640]{3,2,1,0:T(8,128)(2,1)S(1)}, bf16[4,4,40,640]{3,2,1,0:T(8,128)(2,1)}, u32[]{:S(2)}) copy-start(bf16[4,4,40,640]{3,2,1,0:T(8,128)(2,1)} %get-tuple-element.15) | copy-start | bytes 2457604
  56.8 14.7 %collective-permute-start.2 = (bf16[64,6400]{1,0:T(8,128)(2,1)}, bf16[64,6400]{1,0:T(8,128)(2,1)}, u32[]{:S(2)}, u32[]{:S(2)}) collective-permute-start(bf16[64,6400]{1,0:T(8,128)(2,1)} %convolution_convert_fusion), channel_id=1, source_target_pairs={{0,12},{1,13},{2,14},{3,15},{4,0},{5,1},{6,2},{7,3},{8,4},{9,5},{1... | collective-permute-start | bytes 2457608 | tf_op jit(solution)/shard_map/ppermute | solution.py:217
  61.8 23.3 %all-to-all-start.2 = ((bf16[4,4,40,640]{3,2,1,0:T(8,128)(2,1)}), bf16[4,4,40,640]{3,2,1,0:T(8,128)(2,1)S(1)}, u32[]{:S(2)}, u32[]{:S(2)}) async-start(bf16[4,4,40,640]{3,2,1,0:T(8,128)(2,1)} %add_convert_fusion), calls=%async_computation.2 | async-start | bytes 1638400 | tf_op jit(solution)/shard_map/all_to_all | solution.py:188
  73.6 23.7 %collective-permute-start.3 = (bf16[16,6400]{1,0:T(8,128)(2,1)S(1)}, bf16[16,6400]{1,0:T(8,128)(2,1)S(1)}, u32[]{:S(2)}, u32[]{:S(2)}) collective-permute-start(bf16[16,6400]{1,0:T(8,128)(2,1)S(1)} %get-tuple-element.20), channel_id=1, source_target_pairs={{0,1},{1,2},{2,3},{3,0},{4,5},{5,6},{6,7},{7,4},{8,9},{9,10},{10,1... | collective-permute-start | bytes 614408 | tf_op jit(solution)/shard_map/ppermute | solution.py:217
  76.0 21.2 %collective-permute-start.4 = (bf16[16,6400]{1,0:T(8,128)(2,1)S(1)}, bf16[16,6400]{1,0:T(8,128)(2,1)S(1)}, u32[]{:S(2)}, u32[]{:S(2)}) collective-permute-start(bf16[16,6400]{1,0:T(8,128)(2,1)S(1)} %get-tuple-element.19), channel_id=1, source_target_pairs={{0,2},{1,3},{2,0},{3,1},{4,6},{5,7},{6,4},{7,5},{8,10},{9,11},{10,... | collective-permute-start | bytes 614408 | tf_op jit(solution)/shard_map/ppermute | solution.py:217
  80.3 17.0 %collective-permute-start.5 = (bf16[16,6400]{1,0:T(8,128)(2,1)S(1)}, bf16[16,6400]{1,0:T(8,128)(2,1)S(1)}, u32[]{:S(2)}, u32[]{:S(2)}) collective-permute-start(bf16[16,6400]{1,0:T(8,128)(2,1)S(1)} %get-tuple-element.18), channel_id=1, source_target_pairs={{0,3},{1,0},{2,1},{3,2},{4,7},{5,4},{6,5},{7,6},{8,11},{9,8},{10,9... | collective-permute-start | bytes 614408 | tf_op jit(solution)/shard_map/ppermute | solution.py:217
  86.0 30.7 %all-to-all-start.3 = ((bf16[4,40,640]{2,1,0:T(8,128)(2,1)}), bf16[4,40,640]{2,1,0:T(8,128)(2,1)S(1)}, u32[]{:S(2)}, u32[]{:S(2)}) async-start(bf16[4,40,640]{2,1,0:T(8,128)(2,1)} %reduce_sum.37), calls=%async_computation.3 | async-start | bytes 409600 | tf_op jit(solution)/shard_map/all_to_all | solution.py:188
where the time goes:
time: 118 us; the launch traced here: 117 us
  starting transfers between devices  53.7 us (46%)
  waiting for transfers between devices  38.7 us (33%)
  Pallas kernels  11.7 us (10%)
  matrix products  5.97 us (5%)
  other arithmetic  4.85 us (4%)
  local copies, waits for them, and re-layouts  1.7 us (1%)
    all_to_all x4, waiting for transfers between devices, exchange(): lax.all_to_all(blocks, axis, 0, 0, tiled=True, axis_index_groups=groups)  35.1 us
    all_to_all x4, starting transfers between devices, exchange(): lax.all_to_all(blocks, axis, 0, 0, tiled=True, axis_index_groups=groups)  31.7 us
    ppermute x6, starting transfers between devices, named_permute(): return lax.ppermute(value, ('dp', 'tp'), pairs)  20.1 us
    dot_general x4, matrix products, route_early(): jnp.dot(table[d * span:(d + 1) * span], part, preferred_element_type=jnp....  5.97 us
    pallas_call x1, Pallas kernels, grad_terms(): pl.pallas_call(functools.partial(grads_kernel, places, factor), out_shape...  4.51 us
    convert_element_type x3, other arithmetic, summed(): sum((b.astype(jnp.float32) for b in moved), own.astype(jnp.float32))  3.92 us
    ppermute x6, waiting for transfers between devices, named_permute(): return lax.ppermute(value, ('dp', 'tp'), pairs)  3.66 us
    pallas_call x1, Pallas kernels, hidden_parts(): pl.pallas_call(functools.partial(hidden_kernel, head), out_shape=(jax.Sha...  3.42 us
  transfers between devices with their start and end apart: 11, of which 4 were waited for; matrix products, arithmetic and copies ran while one was open for 9% of the time, Pallas kernels for 8%

commit v1 on v0

--- a/solution.py
+++ b/solution.py
@@ -10,6 +10,7 @@
 
 SUB, LANE = 8, 128
 SLOT_PAD = 16
+GRADS_VMEM = 24
 
 
 def tile_places(rows, width, parts):
@@ -29,15 +30,16 @@
     return whole + 1, places
 
 
-def cut_kernel(places, x_ref, layer_ref, out_ref):
+def cut_kernel(places, x_hbm, layer_hbm, out_hbm, x_ref, layer_ref, out_ref, in_sem, out_sem):
     parts, depth = out_ref.shape[:2]
     slot_count, width = layer_ref.shape
     across = width // LANE
     head = depth - (SLOT_PAD // SUB) * across
-    for part, i, at, size, r, c in places:
-        out_ref[part, i, at : at + size, :] = x_ref[r : r + size, c : c + LANE]
-        if size < SUB:
-            out_ref[part, i, size:, :] = jnp.zeros((SUB - size, LANE), out_ref.dtype)
+    get_layer = pltpu.make_async_copy(layer_hbm, layer_ref, in_sem.at[0])
+    get_x = pltpu.make_async_copy(x_hbm.at[:, pl.ds(0, width)], x_ref, in_sem.at[1])
+    get_layer.start()
+    get_x.start()
+    get_layer.wait()
     for at in range(0, SLOT_PAD, SUB):
         size = min(SUB, slot_count - at)
         for c in range(across):
@@ -46,18 +48,38 @@
                 out_ref[part, head + (at // SUB) * across + c, :size, :] = tile
                 if size < SUB:
                     out_ref[part, head + (at // SUB) * across + c, size:, :] = jnp.zeros((SUB - size, LANE), tile.dtype)
+    rest = pl.ds(head, depth - head)
+    put_layer = pltpu.make_async_copy(out_ref.at[:, rest], out_hbm.at[:, rest], out_sem.at[0])
+    put_layer.start()
+    get_x.wait()
+    for part, i, at, size, r, c in places:
+        out_ref[part, i, at : at + size, :] = x_ref[r : r + size, c : c + LANE]
+        if size < SUB:
+            out_ref[part, i, size:, :] = jnp.zeros((SUB - size, LANE), out_ref.dtype)
+    some = pl.ds(0, head)
+    put_x = pltpu.make_async_copy(out_ref.at[:, some], out_hbm.at[:, some], out_sem.at[1])
+    put_x.start()
+    put_layer.wait()
+    put_x.wait()
 
 
 def cut_tiles(x, layer, parts):
     rows, width = x.shape[0], layer.shape[1]
     depth, places = tile_places(rows, width, parts)
     depth += (SLOT_PAD // SUB) * (width // LANE)
+    anywhere = pl.BlockSpec(memory_space=pl.ANY)
     return pl.pallas_call(
         functools.partial(cut_kernel, places),
-        grid=(1,),
-        in_specs=[pl.BlockSpec((rows, width), lambda i: (0, 0)), pl.BlockSpec(layer.shape, lambda i: (0, 0))],
-        out_specs=pl.BlockSpec((parts, depth, SUB, LANE), lambda i: (0, 0, 0, 0)),
+        in_specs=[anywhere] * 2,
+        out_specs=anywhere,
         out_shape=jax.ShapeDtypeStruct((parts, depth, SUB, LANE), x.dtype),
+        scratch_shapes=[
+            pltpu.VMEM((rows, width), x.dtype),
+            pltpu.VMEM(layer.shape, x.dtype),
+            pltpu.VMEM((parts, depth, SUB, LANE), x.dtype),
+            pltpu.SemaphoreType.DMA((2,)),
+            pltpu.SemaphoreType.DMA((2,)),
+        ],
         name="cut_tiles",
     )(x, layer)
 
@@ -68,28 +90,29 @@
     return (preact * normal_cdf, normal_cdf + preact * density)
 
 
-def hidden_kernel(head, tiles_ref, gain_ref, bias_ref, weight_ref, fc1_bias_ref, normed_ref, hidden_ref, deriv_ref):
+def hidden_kernel(head, tiles_ref, gain_ref, bias_ref, weight_ref, fc1_bias_ref, packed_ref):
     parts = tiles_ref.shape[0]
-    slots, width = normed_ref.shape
+    slots = packed_ref.shape[0]
+    units, width = weight_ref.shape
+    wide = -(-units // LANE) * LANE
     across = width // LANE
     per_part = slots // parts
     for part in range(parts):
         for at in range(0, per_part, SUB):
             for c in range(across):
-                normed_ref[part * per_part + at : part * per_part + at + SUB, c * LANE : (c + 1) * LANE] = tiles_ref[
+                packed_ref[part * per_part + at : part * per_part + at + SUB, c * LANE : (c + 1) * LANE] = tiles_ref[
                     part, head + (at // SUB) * across + c
                 ]
-    values = normed_ref[...].astype(jnp.float32)
+    values = packed_ref[:, :width].astype(jnp.float32)
     centered = values - jnp.mean(values, axis=1, keepdims=True)
     row_var = jnp.mean(centered * centered, axis=1, keepdims=True)
     normed = (centered / jnp.sqrt(row_var + 1e-05) * gain_ref[...][None] + bias_ref[...][None]).astype(jnp.bfloat16)
-    normed_ref[...] = normed
+    packed_ref[:, :width] = normed
     preact = lax.dot_general(normed, weight_ref[...], (((1,), (1,)), ((), ())), preferred_element_type=jnp.float32)
     activated, derivative = gelu_parts(preact + fc1_bias_ref[...][None])
-    gap = hidden_ref.shape[1] - activated.shape[1]
-    hidden_ref[...] = jnp.zeros_like(hidden_ref)
-    hidden_ref[:, gap:] = activated.astype(jnp.bfloat16)
-    deriv_ref[...] = derivative
+    packed_ref[:, width:] = jnp.zeros((slots, 2 * wide), jnp.bfloat16)
+    packed_ref[:, width + wide - units : width + wide] = activated.astype(jnp.bfloat16)
+    packed_ref[:, width + wide : width + wide + units] = derivative.astype(jnp.bfloat16)
 
 
 def hidden_parts(tiles, head, gain, bias, weight_t, fc1_bias):
@@ -98,34 +121,46 @@
     wide = -(-units // LANE) * LANE
     return pl.pallas_call(
         functools.partial(hidden_kernel, head),
-        out_shape=(
-            jax.ShapeDtypeStruct((slots, width), jnp.bfloat16),
-            jax.ShapeDtypeStruct((slots, wide), jnp.bfloat16),
-            jax.ShapeDtypeStruct((slots, units), jnp.float32),
-        ),
+        out_shape=jax.ShapeDtypeStruct((slots, width + 2 * wide), jnp.bfloat16),
         name="hidden_parts",
     )(tiles, gain, bias, weight_t, fc1_bias)
 
 
-def grads_kernel(places, factor, tiles_ref, table_ref, normed_ref, hidden_ref, deriv_ref, weight_ref, mine_ref, theirs_ref, rows_ref, up_ref, pg_ref):
+def grads_kernel(places, factor, *refs):
+    sources, (mine_hbm, theirs_hbm), scratch = refs[:4], refs[4:6], refs[6:]
+    tiles_ref, table_ref, weight_ref, packed_ref = scratch[:4]
+    mine_ref, theirs_ref, rows_ref, up_ref, pg_ref, in_sem, out_sem = scratch[4:]
+    width = up_ref.shape[1]
+    loads = [pltpu.make_async_copy(src, dst, in_sem.at[i]) for i, (src, dst) in enumerate(zip(sources, scratch[:4]))]
+    for load in loads:
+        load.start()
+    loads[0].wait()
     for part, i, at, size, r, c in places:
         rows_ref[r : r + size, c : c + LANE] = tiles_ref[part, i, at : at + size, :]
+    loads[1].wait()
     up_ref[...] = jnp.dot(table_ref[...], rows_ref[...], preferred_element_type=jnp.float32).astype(jnp.bfloat16)
+    loads[2].wait()
     hidden_grad = lax.dot_general(
         up_ref[...], weight_ref[...], (((1,), (1,)), ((), ())), preferred_element_type=jnp.float32
     )
     units = hidden_grad.shape[1]
+    loads[3].wait()
+    deriv_at = width + pg_ref.shape[1]
     pg_ref[...] = jnp.zeros_like(pg_ref)
-    pg_ref[:, :units] = (hidden_grad * deriv_ref[...]).astype(jnp.bfloat16)
-    near, _, block, _ = mine_ref.shape
+    pg_ref[:, :units] = (hidden_grad * packed_ref[:, deriv_at : deriv_at + units].astype(jnp.float32)).astype(jnp.bfloat16)
+    near, far, block, _ = mine_ref.shape
     wide = pg_ref.shape[1]
     keep = wide - LANE
-    step = 5 * LANE
+    halves = 2
+    step = width // halves
     low = lax.axis_index("dp") % 2 == 0
-    for at in range(0, normed_ref.shape[1], step):
+    stores = []
+    for turn in range(halves):
+        at = turn * step
         dims = (((0,), (0,)), ((), ()))
-        first = lax.dot_general(normed_ref[:, at : at + step], pg_ref[...], dims, preferred_element_type=jnp.float32)
-        second = lax.dot_general(up_ref[:, at : at + step], hidden_ref[...], dims, preferred_element_type=jnp.float32)
+        first = lax.dot_general(packed_ref[:, at : at + step], pg_ref[...], dims, preferred_element_type=jnp.float32)
+        hidden = packed_ref[:, width : width + wide]
+        second = lax.dot_general(up_ref[:, at : at + step], hidden, dims, preferred_element_type=jnp.float32)
         for b in range(0, step, 2 * block):
             m, p = divmod((at + b) // (2 * block), near)
             parts = []
@@ -135,22 +170,40 @@
             for lo, hi, start in zip(*parts, (0, keep, wide)):
                 mine_ref[p, m, :, start : start + lo.shape[1]] = jnp.where(low, lo, hi).astype(jnp.bfloat16)
                 theirs_ref[p, m, :, start : start + lo.shape[1]] = jnp.where(low, hi, lo).astype(jnp.bfloat16)
-
-
-def grad_terms(tiles, table, normed, hidden, deriv, weight_t, factor, shape):
-    slots, width = normed.shape
-    rows = table.shape[1]
+        some = pl.ds(turn * (far // halves), far // halves)
+        for j, (src, dst) in enumerate(((theirs_ref, theirs_hbm), (mine_ref, mine_hbm))):
+            store = pltpu.make_async_copy(src.at[:, some], dst.at[:, some], out_sem.at[2 * turn + j])
+            store.start()
+            stores.append(store)
+    for store in stores:
+        store.wait()
+
+
+def grad_terms(tiles, table, packed, weight_t, factor, shape):
+    units, width = weight_t.shape
+    slots, rows = table.shape
+    wide = -(-units // LANE) * LANE
     _, places = tile_places(rows, width, tiles.shape[0])
+    operands = (tiles, table, weight_t, packed)
+    anywhere = pl.BlockSpec(memory_space=pl.ANY)
     return pl.pallas_call(
         functools.partial(grads_kernel, places, factor),
+        in_specs=[anywhere] * len(operands),
+        out_specs=(anywhere,) * 2,
         out_shape=(jax.ShapeDtypeStruct(shape, jnp.bfloat16),) * 2,
-        scratch_shapes=[
+        scratch_shapes=[pltpu.VMEM(a.shape, a.dtype) for a in operands]
+        + [
+            pltpu.VMEM(shape, jnp.bfloat16),
+            pltpu.VMEM(shape, jnp.bfloat16),
             pltpu.VMEM((rows, width), jnp.bfloat16),
             pltpu.VMEM((slots, width), jnp.bfloat16),
-            pltpu.VMEM((slots, hidden.shape[1]), jnp.bfloat16),
+            pltpu.VMEM((slots, wide), jnp.bfloat16),
+            pltpu.SemaphoreType.DMA((len(operands),)),
+            pltpu.SemaphoreType.DMA((4,)),
         ],
         name="grad_terms",
-    )(tiles, table, normed, hidden, deriv, weight_t)
+        compiler_params=pltpu.CompilerParams(vmem_limit_bytes=GRADS_VMEM << 20),
+    )(*operands)
 
 
 def tables_kernel(side, ranks_ref, table_ref, early_ref):
@@ -267,12 +320,12 @@
     tiles = to_all(own_tiles, "tp")
 
     table, early_table = slot_tables(row_rank.T, groups)
-    normed_all, hidden, derivative = hidden_parts(arrived, head, ln_gain, ln_bias, fc1_weight.T, fc1_bias)
+    packed = hidden_parts(arrived, head, ln_gain, ln_bias, fc1_weight.T, fc1_bias)
     placed = route_early(local_part[:, width:], early_table, replicas, groups)[:slot_count]
 
     factor = float(replicas * row_count) ** (-0.5)
     mine, theirs = grad_terms(
-        tiles, table, normed_all, hidden, derivative, fc2_weight.T, factor,
+        tiles, table, packed, fc2_weight.T, factor,
         (near, far, block, 2 * units),
     )
     theirs = lax.ppermute(theirs, "dp", pairs)
@@ -281,7 +334,8 @@
     both = total(both)
     both = exchange(both, "dp", strided)
     both = total(both)
-    return (placed, both[:, :units], both[:, units:])
+    first, second = both[:, :units], both[:, units:]
+    return (placed, first, second)
 
 
 def solution(mesh):

time: 118 us -> 118 us (level)
  Pallas kernels: 11.7 us -> 10.1 us
    pallas_call x3, Pallas kernels: 10.1 us -> 8.46 us  [the longest x1 3.57 us: hidden_parts(): pl.pallas_call(functools.partial(hidden_kernel, head), out_shape=jax.Shap...]
    unnamed x8 -> x12, local copies, waits for them, and re-layouts: 0.02 us -> 1.24 us
  transfers between devices with their start and end apart: 11 -> 11, of which waited for: 4 -> 4; matrix products, arithmetic and copies ran while one was open for 9% -> 9% of each run, Pallas kernels for 8% -> 7%
where the time goes in v1:
time: 118 us; the launch traced here: 117 us
  starting transfers between devices  53 us (45%)
  waiting for transfers between devices  38.7 us (33%)
  Pallas kernels  10.1 us (9%)
  other arithmetic  5.9 us (5%)
  matrix products  5.88 us (5%)
  local copies, waits for them, and re-layouts  2.82 us (2%)
    all_to_all x4, waiting for transfers between devices, exchange(): lax.all_to_all(blocks, axis, 0, 0, tiled=True, axis_index_groups=groups)  35.3 us
    all_to_all x4, starting transfers between devices, exchange(): lax.all_to_all(blocks, axis, 0, 0, tiled=True, axis_index_groups=groups)  30.9 us
    ppermute x6, starting transfers between devices, named_permute(): return lax.ppermute(value, ('dp', 'tp'), pairs)  20.1 us
    dot_general x4, matrix products, route_early(): jnp.dot(table[d * span:(d + 1) * span], part, preferred_element_type=jnp....  5.88 us
    convert_element_type x3, other arithmetic, summed(): sum((b.astype(jnp.float32) for b in moved), own.astype(jnp.float32))  3.96 us
    pallas_call x1, Pallas kernels, hidden_parts(): pl.pallas_call(functools.partial(hidden_kernel, head), out_shape=jax.Shap...  3.57 us
    ppermute x6, waiting for transfers between devices, named_permute(): return lax.ppermute(value, ('dp', 'tp'), pairs)  3.43 us
    pallas_call x1, Pallas kernels, grad_terms(): pl.pallas_call(functools.partial(grads_kernel, places, factor), in_specs=...  2.88 us
  transfers between devices with their start and end apart: 11, of which 4 were waited for; matrix products, arithmetic and copies ran while one was open for 9% of the time, Pallas kernels for 7%

profile of v1, /device:TPU:56, one launch (start us, length us, event | category | flops | bytes accessed | tf_op | source)
XLA Modules:
  0.0 117.2 jit_solution(8285301093990260904)
XLA Ops:
  0.6 2.0 %cut_tiles.1 = bf16[16,33,8,128]{3,2,1,0:T(8,128)(2,1)} custom-call(bf16[160,7680]{1,0:T(8,128)(2,1)} %bitcast.5, bf16[15,1280]{1,0:T(8,128)(2,1)} %layer_hbm.1), custom_call_target="tpu_custom_call" | custom-call | tf_op jit(solution)/shard_map/cut_tiles/pallas_call | solution.py:71
  2.7 7.3 %all-to-all-start = ((bf16[16,33,8,128]{3,2,1,0:T(8,128)(2,1)}), bf16[16,33,8,128]{3,2,1,0:T(8,128)(2,1)}, u32[]{:S(2)}, u32[]{:S(2)}) async-start(bf16[16,33,8,128]{3,2,1,0:T(8,128)(2,1)} %cut_tiles.1), calls=%async_computation | async-start | bytes 2162688 | tf_op jit(solution)/shard_map/all_to_all | solution.py:241
  10.0 1.6 %slot_tables.1 = (bf16[256,160]{1,0:T(8,128)(2,1)}, bf16[256,160]{1,0:T(8,128)(2,1)}) custom-call(s32[1,160]{1,0:T(1,128)} %bitcast.11), custom_call_target="tpu_custom_call" | custom-call | tf_op jit(solution)/shard_map/slot_tables/pallas_call | solution.py:235
  11.6 13.7 %all-to-all-done.tiles_ref = bf16[16,33,8,128]{3,2,1,0:T(8,128)(2,1)} async-done(((bf16[16,33,8,128]{3,2,1,0:T(8,128)(2,1)}), bf16[16,33,8,128]{3,2,1,0:T(8,128)(2,1)}, u32[]{:S(2)}, u32[]{:S(2)}) %all-to-all-start) | async-done | bytes 1081376 | tf_op jit(solution)/shard_map/all_to_all | solution.py:241
  25.2 1.1 slice_reduce_fusion
  26.3 0.8 broadcast_in_dim.3
  27.1 6.5 %all-to-all-start.1 = ((bf16[16,13,8,128]{3,2,1,0:T(8,128)(2,1)}), bf16[16,13,8,128]{3,2,1,0:T(8,128)(2,1)S(1)}, u32[]{:S(2)}, u32[]{:S(2)}) async-start(bf16[16,13,8,128]{3,2,1,0:T(8,128)(2,1)} %broadcast_in_dim.3), calls=%async_computation.1 | async-start | bytes 851968 | tf_op jit(solution)/shard_map/all_to_all | solution.py:241
  33.6 2.1 %convolution_convert_fusion.2 = bf16[64,6400]{1,0:T(8,128)(2,1)} fusion(bf16[160,7680]{1,0:T(8,128)(2,1)S(1)} %bitcast.7, bf16[256,160]{1,0:T(8,128)(2,1)} %get-tuple-element.7), kind=kOutput, calls=%fused_computation.2 | convolution fusion | flops 131481600 | bytes 2899968 | tf_op jit(solution)/shard_map/dot_general | solution.py:283
  35.7 3.4 %collective-permute-start = (bf16[64,6400]{1,0:T(8,128)(2,1)}, bf16[64,6400]{1,0:T(8,128)(2,1)}, u32[]{:S(2)}, u32[]{:S(2)}) collective-permute-start(bf16[64,6400]{1,0:T(8,128)(2,1)} %convolution_convert_fusion.2), channel_id=1, source_target_pairs={{0,4},{1,5},{2,6},{3,7},{4,8},{5,9},{6,10},{7,11},{8,12},{9,13},{1... | collective-permute-start | bytes 2457608 | tf_op jit(solution)/shard_map/ppermute | solution.py:270
  39.1 1.4 %convolution_convert_fusion.1 = bf16[64,6400]{1,0:T(8,128)(2,1)} fusion(bf16[160,7680]{1,0:T(8,128)(2,1)S(1)} %bitcast.8, bf16[256,160]{1,0:T(8,128)(2,1)S(1)} %copy-done.5), kind=kOutput, calls=%fused_computation.1 | convolution fusion | flops 131481600 | bytes 2899968 | tf_op jit(solution)/shard_map/dot_general | solution.py:283
  40.5 4.8 %collective-permute-start.1 = (bf16[64,6400]{1,0:T(8,128)(2,1)}, bf16[64,6400]{1,0:T(8,128)(2,1)}, u32[]{:S(2)}, u32[]{:S(2)}) collective-permute-start(bf16[64,6400]{1,0:T(8,128)(2,1)} %convolution_convert_fusion.1), channel_id=1, source_target_pairs={{0,8},{1,9},{2,10},{3,11},{4,12},{5,13},{6,14},{7,15},{8,0},{9,1},... | collective-permute-start | bytes 2457608 | tf_op jit(solution)/shard_map/ppermute | solution.py:270
  45.3 3.6 %hidden_parts.1.refs_3_ = bf16[256,2048]{1,0:T(8,128)(2,1)} custom-call(bf16[16,33,8,128]{3,2,1,0:T(8,128)(2,1)} %all-to-all-done.tiles_ref, f32[1280]{0:T(1024)} %gain_ref.1, f32[1280]{0:T(1024)} %bias_ref.1, bf16[320,1280]{1,0:T(8,128)(2,1)} %bitcast.10, f32[320]{0:T(512)} %fc1_bias_ref.1), custom_call_target="tpu_custom_call" | custom-call | tf_op jit(solution)/shard_map/hidden_parts/pallas_call | solution.py:122
  48.8 1.2 %copy-done = bf16[256,2048]{1,0:T(8,128)(2,1)S(1)} copy-done((bf16[256,2048]{1,0:T(8,128)(2,1)S(1)}, bf16[256,2048]{1,0:T(8,128)(2,1)}, u32[]{:S(2)}) %copy-start) | copy-done | bytes 1048600
  50.1 2.9 %grad_terms.1 = (bf16[4,4,40,640]{3,2,1,0:T(8,128)(2,1)S(1)}, bf16[4,4,40,640]{3,2,1,0:T(8,128)(2,1)S(1)}) custom-call(bf16[16,13,8,128]{3,2,1,0:T(8,128)(2,1)S(1)} %all-to-all-done.1.refs_0_, bf16[256,160]{1,0:T(8,128)(2,1)S(1)} %copy-done.2, bf16[320,1280]{1,0:T(8,128)(2,1)S(1)} %bitcast.4, bf16[256,2048]{1,0:T(8,128)(2,1)S(1)} %copy-done), custom_call_target="tpu_custom_call" | custom-call | tf_op jit(solution)/shard_map/grad_terms/pallas_call | solution.py:189
  53.0 2.1 %collective-permute-start.6 = (bf16[4,4,40,640]{3,2,1,0:T(8,128)(2,1)S(1)}, bf16[4,4,40,640]{3,2,1,0:T(8,128)(2,1)S(1)}, u32[]{:S(2)}, u32[]{:S(2)}) collective-permute-start(bf16[4,4,40,640]{3,2,1,0:T(8,128)(2,1)S(1)} %get-tuple-element.10), channel_id=1, source_target_pairs={{0,16},{16,0},{32,48},{48,32},{64,80},{80,64},{96,112},{112,96},{1... | collective-permute-start | bytes 2457608 | tf_op jit(solution)/shard_map/ppermute | solution.py:331
  55.0 2.0 %convolution_convert_fusion = bf16[64,6400]{1,0:T(8,128)(2,1)S(1)} fusion(bf16[160,7680]{1,0:T(8,128)(2,1)} %bitcast.6, bf16[256,160]{1,0:T(8,128)(2,1)S(1)} %copy-done.5), kind=kOutput, calls=%fused_computation | convolution fusion | flops 131481600 | bytes 2899968 | tf_op jit(solution)/shard_map/dot_general | solution.py:283
  57.0 3.3 %collective-permute-start.2 = (bf16[64,6400]{1,0:T(8,128)(2,1)S(1)}, bf16[64,6400]{1,0:T(8,128)(2,1)}, u32[]{:S(2)}, u32[]{:S(2)}) collective-permute-start(bf16[64,6400]{1,0:T(8,128)(2,1)S(1)} %convolution_convert_fusion), channel_id=1, source_target_pairs={{0,12},{1,13},{2,14},{3,15},{4,0},{5,1},{6,2},{7,3},{8,4},{9,5},{1... | collective-permute-start | bytes 2457608 | tf_op jit(solution)/shard_map/ppermute | solution.py:270
  60.4 0.4 convolution_convert_fusion.3
  60.8 1.1 add_convert_fusion
  61.9 6.0 %all-to-all-start.2 = ((bf16[4,4,40,640]{3,2,1,0:T(8,128)(2,1)}), bf16[4,4,40,640]{3,2,1,0:T(8,128)(2,1)S(1)}, u32[]{:S(2)}, u32[]{:S(2)}) async-start(bf16[4,4,40,640]{3,2,1,0:T(8,128)(2,1)} %add_convert_fusion), calls=%async_computation.2 | async-start | bytes 1638400 | tf_op jit(solution)/shard_map/all_to_all | solution.py:241
  68.0 3.4 %collective-permute-done.2 = bf16[64,6400]{1,0:T(8,128)(2,1)} collective-permute-done((bf16[64,6400]{1,0:T(8,128)(2,1)S(1)}, bf16[64,6400]{1,0:T(8,128)(2,1)}, u32[]{:S(2)}, u32[]{:S(2)}) %collective-permute-start.2) | collective-permute-done | bytes 819232 | tf_op jit(solution)/shard_map/ppermute | solution.py:270
  71.4 2.0 %add_convert_fusion.1 = bf16[64,6400]{1,0:T(8,128)(2,1)S(1)} fusion(bf16[64,6400]{1,0:T(8,128)(2,1)} %collective-permute-done.2, bf16[64,6400]{1,0:T(8,128)(2,1)} %collective-permute-done.1, bf16[64,6400]{1,0:T(8,128)(2,1)} %collective-permute-done, bf16[64,6400]{1,0:T(8,128)(2,1)S(1)} %convolution_convert_fusion.3), kind=kLoop, calls=%fused_computation.5 | loop fusion | flops 3276800 | bytes 4096000 | tf_op jit(solution)/shard_map/convert_element_type | solution.py:274
  73.4 0.1 fusion.8
  73.5 2.4 %collective-permute-start.3 = (bf16[16,6400]{1,0:T(8,128)(2,1)S(1)}, bf16[16,6400]{1,0:T(8,128)(2,1)S(1)}, u32[]{:S(2)}, u32[]{:S(2)}) collective-permute-start(bf16[16,6400]{1,0:T(8,128)(2,1)S(1)} %get-tuple-element.14), channel_id=1, source_target_pairs={{0,1},{1,2},{2,3},{3,0},{4,5},{5,6},{6,7},{7,4},{8,9},{9,10},{10,1... | collective-permute-start | bytes 614408 | tf_op jit(solution)/shard_map/ppermute | solution.py:270
  75.9 4.3 %collective-permute-start.4 = (bf16[16,6400]{1,0:T(8,128)(2,1)S(1)}, bf16[16,6400]{1,0:T(8,128)(2,1)S(1)}, u32[]{:S(2)}, u32[]{:S(2)}) collective-permute-start(bf16[16,6400]{1,0:T(8,128)(2,1)S(1)} %get-tuple-element.13), channel_id=1, source_target_pairs={{0,2},{1,3},{2,0},{3,1},{4,6},{5,7},{6,4},{7,5},{8,10},{9,11},{10,... | collective-permute-start | bytes 614408 | tf_op jit(solution)/shard_map/ppermute | solution.py:270
  80.2 1.9 %collective-permute-start.5 = (bf16[16,6400]{1,0:T(8,128)(2,1)S(1)}, bf16[16,6400]{1,0:T(8,128)(2,1)S(1)}, u32[]{:S(2)}, u32[]{:S(2)}) collective-permute-start(bf16[16,6400]{1,0:T(8,128)(2,1)S(1)} %get-tuple-element.12), channel_id=1, source_target_pairs={{0,3},{1,0},{2,1},{3,2},{4,7},{5,4},{6,5},{7,6},{8,11},{9,8},{10,9... | collective-permute-start | bytes 614408 | tf_op jit(solution)/shard_map/ppermute | solution.py:270
  82.1 3.1 %all-to-all-done.2 = bf16[4,4,40,640]{3,2,1,0:T(8,128)(2,1)S(1)} async-done(((bf16[4,4,40,640]{3,2,1,0:T(8,128)(2,1)}), bf16[4,4,40,640]{3,2,1,0:T(8,128)(2,1)S(1)}, u32[]{:S(2)}, u32[]{:S(2)}) %all-to-all-start.2) | async-done | bytes 819232 | tf_op jit(solution)/shard_map/all_to_all | solution.py:241
  85.2 0.8 reduce_sum.37
  86.1 11.1 %all-to-all-start.3 = ((bf16[4,40,640]{2,1,0:T(8,128)(2,1)}), bf16[4,40,640]{2,1,0:T(8,128)(2,1)S(1)}, u32[]{:S(2)}, u32[]{:S(2)}) async-start(bf16[4,40,640]{2,1,0:T(8,128)(2,1)} %reduce_sum.37), calls=%async_computation.3 | async-start | bytes 409600 | tf_op jit(solution)/shard_map/all_to_all | solution.py:241
  97.2 0.8 add_convert_fusion.2
  98.0 18.5 %all-to-all-done.3 = bf16[4,40,640]{2,1,0:T(8,128)(2,1)S(1)} async-done(((bf16[4,40,640]{2,1,0:T(8,128)(2,1)}), bf16[4,40,640]{2,1,0:T(8,128)(2,1)S(1)}, u32[]{:S(2)}, u32[]{:S(2)}) %all-to-all-start.3) | async-done | bytes 204832 | tf_op jit(solution)/shard_map/all_to_all | solution.py:241
  116.5 0.7 fusion.9
  (19 shorter events, 0.1 us)
Async XLA Ops:
  2.6 31.0 %copy-start.3 = (bf16[1,160,7680]{2,1,0:T(8,128)(2,1)S(1)}, bf16[1,160,7680]{2,1,0:T(8,128)(2,1)}, u32[]{:S(2)}) copy-start(bf16[1,160,7680]{2,1,0:T(8,128)(2,1)} %param.8) | copy-start | bytes 7372804
  2.7 22.6 %all-to-all-start = ((bf16[16,33,8,128]{3,2,1,0:T(8,128)(2,1)}), bf16[16,33,8,128]{3,2,1,0:T(8,128)(2,1)}, u32[]{:S(2)}, u32[]{:S(2)}) async-start(bf16[16,33,8,128]{3,2,1,0:T(8,128)(2,1)} %cut_tiles.1), calls=%async_computation | async-start | bytes 2162688 | tf_op jit(solution)/shard_map/all_to_all | solution.py:241
  26.3 12.8 %copy-start.5 = (bf16[256,160]{1,0:T(8,128)(2,1)S(1)}, bf16[256,160]{1,0:T(8,128)(2,1)}, u32[]{:S(2)}) copy-start(bf16[256,160]{1,0:T(8,128)(2,1)} %get-tuple-element.7) | copy-start | bytes 245764
  27.1 21.7 %all-to-all-start.1 = ((bf16[16,13,8,128]{3,2,1,0:T(8,128)(2,1)}), bf16[16,13,8,128]{3,2,1,0:T(8,128)(2,1)S(1)}, u32[]{:S(2)}, u32[]{:S(2)}) async-start(bf16[16,13,8,128]{3,2,1,0:T(8,128)(2,1)} %broadcast_in_dim.3), calls=%async_computation.1 | async-start | bytes 851968 | tf_op jit(solution)/shard_map/all_to_all | solution.py:241
  35.7 32.3 %collective-permute-start = (bf16[64,6400]{1,0:T(8,128)(2,1)}, bf16[64,6400]{1,0:T(8,128)(2,1)}, u32[]{:S(2)}, u32[]{:S(2)}) collective-permute-start(bf16[64,6400]{1,0:T(8,128)(2,1)} %convolution_convert_fusion.2), channel_id=1, source_target_pairs={{0,4},{1,5},{2,6},{3,7},{4,8},{5,9},{6,10},{7,11},{8,12},{9,13},{1... | collective-permute-start | bytes 2457608 | tf_op jit(solution)/shard_map/ppermute | solution.py:270
  40.5 8.3 %copy-start.1 = (bf16[1280,320]{0,1:T(8,128)(2,1)S(1)}, bf16[1280,320]{0,1:T(8,128)(2,1)}, u32[]{:S(2)}) copy-start(bf16[1280,320]{0,1:T(8,128)(2,1)} %param.14) | copy-start | bytes 2457604
  40.5 8.3 %copy-start.2 = (bf16[256,160]{1,0:T(8,128)(2,1)S(1)}, bf16[256,160]{1,0:T(8,128)(2,1)}, u32[]{:S(2)}) copy-start(bf16[256,160]{1,0:T(8,128)(2,1)} %get-tuple-element.8.refs_1_) | copy-start | bytes 245764
  40.5 27.5 %collective-permute-start.1 = (bf16[64,6400]{1,0:T(8,128)(2,1)}, bf16[64,6400]{1,0:T(8,128)(2,1)}, u32[]{:S(2)}, u32[]{:S(2)}) collective-permute-start(bf16[64,6400]{1,0:T(8,128)(2,1)} %convolution_convert_fusion.1), channel_id=1, source_target_pairs={{0,8},{1,9},{2,10},{3,11},{4,12},{5,13},{6,14},{7,15},{8,0},{9,1},... | collective-permute-start | bytes 2457608 | tf_op jit(solution)/shard_map/ppermute | solution.py:270
  48.8 1.2 %copy-start = (bf16[256,2048]{1,0:T(8,128)(2,1)S(1)}, bf16[256,2048]{1,0:T(8,128)(2,1)}, u32[]{:S(2)}) copy-start(bf16[256,2048]{1,0:T(8,128)(2,1)} %hidden_parts.1.refs_3_) | copy-start | bytes 3145732
  52.9 7.4 %copy-start.4 = (bf16[1,160,7680]{2,1,0:T(8,128)(2,1)S(1)}, bf16[1,160,7680]{2,1,0:T(8,128)(2,1)}, u32[]{:S(2)}) copy-start(bf16[1,160,7680]{2,1,0:T(8,128)(2,1)} %param.8) | copy-start | bytes 7372804
  53.0 7.8 %collective-permute-start.6 = (bf16[4,4,40,640]{3,2,1,0:T(8,128)(2,1)S(1)}, bf16[4,4,40,640]{3,2,1,0:T(8,128)(2,1)S(1)}, u32[]{:S(2)}, u32[]{:S(2)}) collective-permute-start(bf16[4,4,40,640]{3,2,1,0:T(8,128)(2,1)S(1)} %get-tuple-element.10), channel_id=1, source_target_pairs={{0,16},{16,0},{32,48},{48,32},{64,80},{80,64},{96,112},{112,96},{1... | collective-permute-start | bytes 2457608 | tf_op jit(solution)/shard_map/ppermute | solution.py:331
  57.0 14.3 %collective-permute-start.2 = (bf16[64,6400]{1,0:T(8,128)(2,1)S(1)}, bf16[64,6400]{1,0:T(8,128)(2,1)}, u32[]{:S(2)}, u32[]{:S(2)}) collective-permute-start(bf16[64,6400]{1,0:T(8,128)(2,1)S(1)} %convolution_convert_fusion), channel_id=1, source_target_pairs={{0,12},{1,13},{2,14},{3,15},{4,0},{5,1},{6,2},{7,3},{8,4},{9,5},{1... | collective-permute-start | bytes 2457608 | tf_op jit(solution)/shard_map/ppermute | solution.py:270
  61.9 23.3 %all-to-all-start.2 = ((bf16[4,4,40,640]{3,2,1,0:T(8,128)(2,1)}), bf16[4,4,40,640]{3,2,1,0:T(8,128)(2,1)S(1)}, u32[]{:S(2)}, u32[]{:S(2)}) async-start(bf16[4,4,40,640]{3,2,1,0:T(8,128)(2,1)} %add_convert_fusion), calls=%async_computation.2 | async-start | bytes 1638400 | tf_op jit(solution)/shard_map/all_to_all | solution.py:241
  73.5 23.7 %collective-permute-start.3 = (bf16[16,6400]{1,0:T(8,128)(2,1)S(1)}, bf16[16,6400]{1,0:T(8,128)(2,1)S(1)}, u32[]{:S(2)}, u32[]{:S(2)}) collective-permute-start(bf16[16,6400]{1,0:T(8,128)(2,1)S(1)} %get-tuple-element.14), channel_id=1, source_target_pairs={{0,1},{1,2},{2,3},{3,0},{4,5},{5,6},{6,7},{7,4},{8,9},{9,10},{10,1... | collective-permute-start | bytes 614408 | tf_op jit(solution)/shard_map/ppermute | solution.py:270
  75.9 21.2 %collective-permute-start.4 = (bf16[16,6400]{1,0:T(8,128)(2,1)S(1)}, bf16[16,6400]{1,0:T(8,128)(2,1)S(1)}, u32[]{:S(2)}, u32[]{:S(2)}) collective-permute-start(bf16[16,6400]{1,0:T(8,128)(2,1)S(1)} %get-tuple-element.13), channel_id=1, source_target_pairs={{0,2},{1,3},{2,0},{3,1},{4,6},{5,7},{6,4},{7,5},{8,10},{9,11},{10,... | collective-permute-start | bytes 614408 | tf_op jit(solution)/shard_map/ppermute | solution.py:270
  80.2 17.0 %collective-permute-start.5 = (bf16[16,6400]{1,0:T(8,128)(2,1)S(1)}, bf16[16,6400]{1,0:T(8,128)(2,1)S(1)}, u32[]{:S(2)}, u32[]{:S(2)}) collective-permute-start(bf16[16,6400]{1,0:T(8,128)(2,1)S(1)} %get-tuple-element.12), channel_id=1, source_target_pairs={{0,3},{1,0},{2,1},{3,2},{4,7},{5,4},{6,5},{7,6},{8,11},{9,8},{10,9... | collective-permute-start | bytes 614408 | tf_op jit(solution)/shard_map/ppermute | solution.py:270
  86.1 30.4 %all-to-all-start.3 = ((bf16[4,40,640]{2,1,0:T(8,128)(2,1)}), bf16[4,40,640]{2,1,0:T(8,128)(2,1)S(1)}, u32[]{:S(2)}, u32[]{:S(2)}) async-start(bf16[4,40,640]{2,1,0:T(8,128)(2,1)} %reduce_sum.37), calls=%async_computation.3 | async-start | bytes 409600 | tf_op jit(solution)/shard_map/all_to_all | solution.py:241

commit v2 on v1

--- a/solution.py
+++ b/solution.py
@@ -90,7 +90,7 @@
     return (preact * normal_cdf, normal_cdf + preact * density)
 
 
-def hidden_kernel(head, tiles_ref, gain_ref, bias_ref, weight_ref, fc1_bias_ref, packed_ref):
+def hidden_kernel(head, tiles_ref, gain_ref, bias_ref, weight_ref, fc1_bias_ref, table_ref, packed_ref):
     parts = tiles_ref.shape[0]
     slots = packed_ref.shape[0]
     units, width = weight_ref.shape
@@ -110,41 +110,45 @@
     packed_ref[:, :width] = normed
     preact = lax.dot_general(normed, weight_ref[...], (((1,), (1,)), ((), ())), preferred_element_type=jnp.float32)
     activated, derivative = gelu_parts(preact + fc1_bias_ref[...][None])
-    packed_ref[:, width:] = jnp.zeros((slots, 2 * wide), jnp.bfloat16)
+    packed_ref[:, width:] = jnp.zeros((slots, packed_ref.shape[1] - width), jnp.bfloat16)
+    packed_ref[:, width + 2 * wide : width + 2 * wide + table_ref.shape[1]] = table_ref[...]
     packed_ref[:, width + wide - units : width + wide] = activated.astype(jnp.bfloat16)
     packed_ref[:, width + wide : width + wide + units] = derivative.astype(jnp.bfloat16)
 
 
-def hidden_parts(tiles, head, gain, bias, weight_t, fc1_bias):
+def hidden_parts(tiles, head, gain, bias, weight_t, fc1_bias, table):
     units, width = weight_t.shape
     slots = tiles.shape[0] * SLOT_PAD
     wide = -(-units // LANE) * LANE
+    spare = -(-table.shape[1] // LANE) * LANE
     return pl.pallas_call(
         functools.partial(hidden_kernel, head),
-        out_shape=jax.ShapeDtypeStruct((slots, width + 2 * wide), jnp.bfloat16),
+        out_shape=jax.ShapeDtypeStruct((slots, width + 2 * wide + spare), jnp.bfloat16),
         name="hidden_parts",
-    )(tiles, gain, bias, weight_t, fc1_bias)
+        compiler_params=pltpu.CompilerParams(vmem_limit_bytes=16 << 20),
+    )(tiles, gain, bias, weight_t, fc1_bias, table)
 
 
 def grads_kernel(places, factor, *refs):
-    sources, (mine_hbm, theirs_hbm), scratch = refs[:4], refs[4:6], refs[6:]
-    tiles_ref, table_ref, weight_ref, packed_ref = scratch[:4]
-    mine_ref, theirs_ref, rows_ref, up_ref, pg_ref, in_sem, out_sem = scratch[4:]
+    sources, (mine_hbm, theirs_hbm), scratch = refs[:3], refs[3:5], refs[5:]
+    tiles_ref, packed_ref, weight_ref = scratch[:3]
+    mine_ref, theirs_ref, rows_ref, up_ref, pg_ref, in_sem, out_sem = scratch[3:]
     width = up_ref.shape[1]
-    loads = [pltpu.make_async_copy(src, dst, in_sem.at[i]) for i, (src, dst) in enumerate(zip(sources, scratch[:4]))]
+    loads = [pltpu.make_async_copy(src, dst, in_sem.at[i]) for i, (src, dst) in enumerate(zip(sources, scratch[:3]))]
     for load in loads:
         load.start()
     loads[0].wait()
     for part, i, at, size, r, c in places:
         rows_ref[r : r + size, c : c + LANE] = tiles_ref[part, i, at : at + size, :]
     loads[1].wait()
-    up_ref[...] = jnp.dot(table_ref[...], rows_ref[...], preferred_element_type=jnp.float32).astype(jnp.bfloat16)
+    table_at = width + 2 * pg_ref.shape[1]
+    table = packed_ref[:, table_at : table_at + rows_ref.shape[0]]
+    up_ref[...] = jnp.dot(table, rows_ref[...], preferred_element_type=jnp.float32).astype(jnp.bfloat16)
     loads[2].wait()
     hidden_grad = lax.dot_general(
         up_ref[...], weight_ref[...], (((1,), (1,)), ((), ())), preferred_element_type=jnp.float32
     )
     units = hidden_grad.shape[1]
-    loads[3].wait()
     deriv_at = width + pg_ref.shape[1]
     pg_ref[...] = jnp.zeros_like(pg_ref)
     pg_ref[:, :units] = (hidden_grad * packed_ref[:, deriv_at : deriv_at + units].astype(jnp.float32)).astype(jnp.bfloat16)
@@ -179,12 +183,12 @@
         store.wait()
 
 
-def grad_terms(tiles, table, packed, weight_t, factor, shape):
+def grad_terms(tiles, packed, weight_t, rows, factor, shape):
     units, width = weight_t.shape
-    slots, rows = table.shape
+    slots = packed.shape[0]
     wide = -(-units // LANE) * LANE
     _, places = tile_places(rows, width, tiles.shape[0])
-    operands = (tiles, table, weight_t, packed)
+    operands = (tiles, packed, weight_t)
     anywhere = pl.BlockSpec(memory_space=pl.ANY)
     return pl.pallas_call(
         functools.partial(grads_kernel, places, factor),
@@ -320,12 +324,12 @@
     tiles = to_all(own_tiles, "tp")
 
     table, early_table = slot_tables(row_rank.T, groups)
-    packed = hidden_parts(arrived, head, ln_gain, ln_bias, fc1_weight.T, fc1_bias)
+    packed = hidden_parts(arrived, head, ln_gain, ln_bias, fc1_weight.T, fc1_bias, table)
     placed = route_early(local_part[:, width:], early_table, replicas, groups)[:slot_count]
 
     factor = float(replicas * row_count) ** (-0.5)
     mine, theirs = grad_terms(
-        tiles, table, packed, fc2_weight.T, factor,
+        tiles, packed, fc2_weight.T, row_count, factor,
         (near, far, block, 2 * units),
     )
     theirs = lax.ppermute(theirs, "dp", pairs)

time: 118 us -> 114 us (0.966)
  Pallas kernels: 10.1 us -> 7.49 us
  other arithmetic: 5.9 us -> 4.59 us
  local copies, waits for them, and re-layouts: 2.82 us -> 1.6 us
    pallas_call x1, Pallas kernels: 3.57 us -> 1.09 us  [hidden_parts(): pl.pallas_call(functools.partial(hidden_kernel, head), out_shape=jax.Shap...]
    unnamed x12 -> x20, local copies, waits for them, and re-layouts: 1.24 us -> 0.04 us
  transfers between devices with their start and end apart: 11 -> 11, of which waited for: 4 -> 4; matrix products, arithmetic and copies ran while one was open for 9% -> 10% of each run, Pallas kernels for 7% -> 5%
where the time goes in v2:
time: 114 us; the launch traced here: 113 us
  starting transfers between devices  52.8 us (46%)
  waiting for transfers between devices  38.8 us (34%)
  Pallas kernels  7.49 us (7%)
  matrix products  6.89 us (6%)
  other arithmetic  4.59 us (4%)
  local copies, waits for them, and re-layouts  1.6 us (1%)
    all_to_all x4, waiting for transfers between devices, exchange(): lax.all_to_all(blocks, axis, 0, 0, tiled=True, axis_index_groups=groups)  35.5 us
    all_to_all x4, starting transfers between devices, exchange(): lax.all_to_all(blocks, axis, 0, 0, tiled=True, axis_index_groups=groups)  30.4 us
    ppermute x6, starting transfers between devices, named_permute(): return lax.ppermute(value, ('dp', 'tp'), pairs)  20.3 us
    dot_general x4, matrix products, route_early(): jnp.dot(table[d * span:(d + 1) * span], part, preferred_element_type=jnp....  6.89 us
    convert_element_type x3, other arithmetic, summed(): sum((b.astype(jnp.float32) for b in moved), own.astype(jnp.float32))  3.68 us
    ppermute x6, waiting for transfers between devices, named_permute(): return lax.ppermute(value, ('dp', 'tp'), pairs)  3.34 us
    pallas_call x1, Pallas kernels, grad_terms(): pl.pallas_call(functools.partial(grads_kernel, places, factor), in_specs=...  2.8 us
  transfers between devices with their start and end apart: 11, of which 4 were waited for; matrix products, arithmetic and copies ran while one was open for 10% of the time, Pallas kernels for 5%

profile of v2, /device:TPU:56, one launch (start us, length us, event | category | flops | bytes accessed | tf_op | source)
XLA Modules:
  0.0 113.1 jit_solution(17199445418587583501)
XLA Ops:
  0.6 2.0 %cut_tiles.1 = bf16[16,33,8,128]{3,2,1,0:T(8,128)(2,1)} custom-call(bf16[160,7680]{1,0:T(8,128)(2,1)} %bitcast.6, bf16[15,1280]{1,0:T(8,128)(2,1)} %layer_hbm.1), custom_call_target="tpu_custom_call" | custom-call | tf_op jit(solution)/shard_map/cut_tiles/pallas_call | solution.py:71
  2.6 7.2 %all-to-all-start = ((bf16[16,33,8,128]{3,2,1,0:T(8,128)(2,1)}), bf16[16,33,8,128]{3,2,1,0:T(8,128)(2,1)S(1)}, u32[]{:S(2)}, u32[]{:S(2)}) async-start(bf16[16,33,8,128]{3,2,1,0:T(8,128)(2,1)} %cut_tiles.1), calls=%async_computation | async-start | bytes 2162688 | tf_op jit(solution)/shard_map/all_to_all | solution.py:245
  9.8 1.6 %slot_tables.1 = (bf16[256,160]{1,0:T(8,128)(2,1)}, bf16[256,160]{1,0:T(8,128)(2,1)}) custom-call(s32[1,160]{1,0:T(1,128)} %bitcast.11), custom_call_target="tpu_custom_call" | custom-call | tf_op jit(solution)/shard_map/slot_tables/pallas_call | solution.py:239
  11.4 13.6 %all-to-all-done.tiles_ref = bf16[16,33,8,128]{3,2,1,0:T(8,128)(2,1)S(1)} async-done(((bf16[16,33,8,128]{3,2,1,0:T(8,128)(2,1)}), bf16[16,33,8,128]{3,2,1,0:T(8,128)(2,1)S(1)}, u32[]{:S(2)}, u32[]{:S(2)}) %all-to-all-start) | async-done | bytes 1081376 | tf_op jit(solution)/shard_map/all_to_all | solution.py:245
  25.0 0.1 slice_reduce_fusion
  25.0 0.8 broadcast_in_dim.3
  25.8 6.5 %all-to-all-start.1 = ((bf16[16,13,8,128]{3,2,1,0:T(8,128)(2,1)}), bf16[16,13,8,128]{3,2,1,0:T(8,128)(2,1)S(1)}, u32[]{:S(2)}, u32[]{:S(2)}) async-start(bf16[16,13,8,128]{3,2,1,0:T(8,128)(2,1)} %broadcast_in_dim.3), calls=%async_computation.1 | async-start | bytes 851968 | tf_op jit(solution)/shard_map/all_to_all | solution.py:245
  32.3 3.1 %convolution_convert_fusion.2 = bf16[64,6400]{1,0:T(8,128)(2,1)} fusion(bf16[160,7680]{1,0:T(8,128)(2,1)} %bitcast.7, bf16[256,160]{1,0:T(8,128)(2,1)S(1)} %copy-done.8), kind=kOutput, calls=%fused_computation.2 | convolution fusion | flops 131481600 | bytes 2899968 | tf_op jit(solution)/shard_map/dot_general | solution.py:287
  35.4 3.5 %collective-permute-start = (bf16[64,6400]{1,0:T(8,128)(2,1)}, bf16[64,6400]{1,0:T(8,128)(2,1)}, u32[]{:S(2)}, u32[]{:S(2)}) collective-permute-start(bf16[64,6400]{1,0:T(8,128)(2,1)} %convolution_convert_fusion.2), channel_id=1, source_target_pairs={{0,4},{1,5},{2,6},{3,7},{4,8},{5,9},{6,10},{7,11},{8,12},{9,13},{1... | collective-permute-start | bytes 2457608 | tf_op jit(solution)/shard_map/ppermute | solution.py:274
  39.0 1.4 %convolution_convert_fusion.1 = bf16[64,6400]{1,0:T(8,128)(2,1)} fusion(bf16[160,7680]{1,0:T(8,128)(2,1)S(1)} %bitcast.9, bf16[256,160]{1,0:T(8,128)(2,1)S(1)} %copy-done.8), kind=kOutput, calls=%fused_computation.1 | convolution fusion | flops 131481600 | bytes 2899968 | tf_op jit(solution)/shard_map/dot_general | solution.py:287
  40.3 4.7 %collective-permute-start.1 = (bf16[64,6400]{1,0:T(8,128)(2,1)}, bf16[64,6400]{1,0:T(8,128)(2,1)}, u32[]{:S(2)}, u32[]{:S(2)}) collective-permute-start(bf16[64,6400]{1,0:T(8,128)(2,1)} %convolution_convert_fusion.1), channel_id=1, source_target_pairs={{0,8},{1,9},{2,10},{3,11},{4,12},{5,13},{6,14},{7,15},{8,0},{9,1},... | collective-permute-start | bytes 2457608 | tf_op jit(solution)/shard_map/ppermute | solution.py:274
  45.1 1.1 hidden_parts.1.refs_1_
  46.2 2.8 %grad_terms.1 = (bf16[4,4,40,640]{3,2,1,0:T(8,128)(2,1)S(1)}, bf16[4,4,40,640]{3,2,1,0:T(8,128)(2,1)S(1)}) custom-call(bf16[16,13,8,128]{3,2,1,0:T(8,128)(2,1)S(1)} %all-to-all-done.1.refs_0_, bf16[256,2304]{1,0:T(8,128)(2,1)S(1)} %hidden_parts.1.refs_1_, bf16[320,1280]{1,0:T(8,128)(2,1)S(1)} %bitcast.5), custom_call_target="tpu_custom_call" | custom-call | tf_op jit(solution)/shard_map/grad_terms/pallas_call | solution.py:193
  49.1 0.0 copy-start.7
  49.1 2.1 %collective-permute-start.6 = (bf16[4,4,40,640]{3,2,1,0:T(8,128)(2,1)S(1)}, bf16[4,4,40,640]{3,2,1,0:T(8,128)(2,1)S(1)}, u32[]{:S(2)}, u32[]{:S(2)}) collective-permute-start(bf16[4,4,40,640]{3,2,1,0:T(8,128)(2,1)S(1)} %get-tuple-element.10), channel_id=1, source_target_pairs={{0,16},{16,0},{32,48},{48,32},{64,80},{80,64},{96,112},{112,96},{1... | collective-permute-start | bytes 2457608 | tf_op jit(solution)/shard_map/ppermute | solution.py:335
  51.1 2.0 %convolution_convert_fusion = bf16[64,6400]{1,0:T(8,128)(2,1)S(1)} fusion(bf16[160,7680]{1,0:T(8,128)(2,1)} %bitcast.8, bf16[256,160]{1,0:T(8,128)(2,1)S(1)} %copy-done.9), kind=kOutput, calls=%fused_computation | convolution fusion | flops 131481600 | bytes 2899968 | tf_op jit(solution)/shard_map/dot_general | solution.py:287
  53.1 3.3 %collective-permute-start.2 = (bf16[64,6400]{1,0:T(8,128)(2,1)S(1)}, bf16[64,6400]{1,0:T(8,128)(2,1)S(1)}, u32[]{:S(2)}, u32[]{:S(2)}) collective-permute-start(bf16[64,6400]{1,0:T(8,128)(2,1)S(1)} %convolution_convert_fusion), channel_id=1, source_target_pairs={{0,12},{1,13},{2,14},{3,15},{4,0},{5,1},{6,2},{7,3},{8,4},{9,5},{1... | collective-permute-start | bytes 2457608 | tf_op jit(solution)/shard_map/ppermute | solution.py:274
  56.5 0.5 convolution_convert_fusion.3
  57.0 1.1 add_convert_fusion
  58.1 6.0 %all-to-all-start.2 = ((bf16[4,4,40,640]{3,2,1,0:T(8,128)(2,1)}), bf16[4,4,40,640]{3,2,1,0:T(8,128)(2,1)S(1)}, u32[]{:S(2)}, u32[]{:S(2)}) async-start(bf16[4,4,40,640]{3,2,1,0:T(8,128)(2,1)} %add_convert_fusion), calls=%async_computation.2 | async-start | bytes 1638400 | tf_op jit(solution)/shard_map/all_to_all | solution.py:245
  64.1 3.3 %collective-permute-done.2 = bf16[64,6400]{1,0:T(8,128)(2,1)S(1)} collective-permute-done((bf16[64,6400]{1,0:T(8,128)(2,1)S(1)}, bf16[64,6400]{1,0:T(8,128)(2,1)S(1)}, u32[]{:S(2)}, u32[]{:S(2)}) %collective-permute-start.2) | collective-permute-done | bytes 819232 | tf_op jit(solution)/shard_map/ppermute | solution.py:274
  67.4 1.8 %add_convert_fusion.1 = bf16[64,6400]{1,0:T(8,128)(2,1)S(1)} fusion(bf16[64,6400]{1,0:T(8,128)(2,1)S(1)} %collective-permute-done.2, bf16[64,6400]{1,0:T(8,128)(2,1)} %collective-permute-done.1, bf16[64,6400]{1,0:T(8,128)(2,1)} %collective-permute-done, bf16[64,6400]{1,0:T(8,128)(2,1)S(1)} %convolution_convert_fusion.3), kind=kLoop, calls=%fused_computation.5 | loop fusion | flops 3276800 | bytes 4096000 | tf_op jit(solution)/shard_map/convert_element_type | solution.py:278
  69.2 0.1 fusion.8
  69.2 2.5 %collective-permute-start.3 = (bf16[16,6400]{1,0:T(8,128)(2,1)S(1)}, bf16[16,6400]{1,0:T(8,128)(2,1)S(1)}, u32[]{:S(2)}, u32[]{:S(2)}) collective-permute-start(bf16[16,6400]{1,0:T(8,128)(2,1)S(1)} %get-tuple-element.14), channel_id=1, source_target_pairs={{0,1},{1,2},{2,3},{3,0},{4,5},{5,6},{6,7},{7,4},{8,9},{9,10},{10,1... | collective-permute-start | bytes 614408 | tf_op jit(solution)/shard_map/ppermute | solution.py:274
  71.7 4.3 %collective-permute-start.4 = (bf16[16,6400]{1,0:T(8,128)(2,1)S(1)}, bf16[16,6400]{1,0:T(8,128)(2,1)S(1)}, u32[]{:S(2)}, u32[]{:S(2)}) collective-permute-start(bf16[16,6400]{1,0:T(8,128)(2,1)S(1)} %get-tuple-element.13), channel_id=1, source_target_pairs={{0,2},{1,3},{2,0},{3,1},{4,6},{5,7},{6,4},{7,5},{8,10},{9,11},{10,... | collective-permute-start | bytes 614408 | tf_op jit(solution)/shard_map/ppermute | solution.py:274
  76.0 1.9 %collective-permute-start.5 = (bf16[16,6400]{1,0:T(8,128)(2,1)S(1)}, bf16[16,6400]{1,0:T(8,128)(2,1)S(1)}, u32[]{:S(2)}, u32[]{:S(2)}) collective-permute-start(bf16[16,6400]{1,0:T(8,128)(2,1)S(1)} %get-tuple-element.12), channel_id=1, source_target_pairs={{0,3},{1,0},{2,1},{3,2},{4,7},{5,4},{6,5},{7,6},{8,11},{9,8},{10,9... | collective-permute-start | bytes 614408 | tf_op jit(solution)/shard_map/ppermute | solution.py:274
  77.9 3.4 %all-to-all-done.2 = bf16[4,4,40,640]{3,2,1,0:T(8,128)(2,1)S(1)} async-done(((bf16[4,4,40,640]{3,2,1,0:T(8,128)(2,1)}), bf16[4,4,40,640]{3,2,1,0:T(8,128)(2,1)S(1)}, u32[]{:S(2)}, u32[]{:S(2)}) %all-to-all-start.2) | async-done | bytes 819232 | tf_op jit(solution)/shard_map/all_to_all | solution.py:245
  81.3 0.8 reduce_sum.37
  82.1 10.8 %all-to-all-start.3 = ((bf16[4,40,640]{2,1,0:T(8,128)(2,1)}), bf16[4,40,640]{2,1,0:T(8,128)(2,1)S(1)}, u32[]{:S(2)}, u32[]{:S(2)}) async-start(bf16[4,40,640]{2,1,0:T(8,128)(2,1)} %reduce_sum.37), calls=%async_computation.3 | async-start | bytes 409600 | tf_op jit(solution)/shard_map/all_to_all | solution.py:245
  93.0 0.8 add_convert_fusion.2
  93.8 18.6 %all-to-all-done.3 = bf16[4,40,640]{2,1,0:T(8,128)(2,1)S(1)} async-done(((bf16[4,40,640]{2,1,0:T(8,128)(2,1)}), bf16[4,40,640]{2,1,0:T(8,128)(2,1)S(1)}, u32[]{:S(2)}, u32[]{:S(2)}) %all-to-all-start.3) | async-done | bytes 204832 | tf_op jit(solution)/shard_map/all_to_all | solution.py:245
  112.4 0.7 fusion.9
  (27 shorter events, 0.1 us)
Async XLA Ops:
  2.6 22.3 %all-to-all-start = ((bf16[16,33,8,128]{3,2,1,0:T(8,128)(2,1)}), bf16[16,33,8,128]{3,2,1,0:T(8,128)(2,1)S(1)}, u32[]{:S(2)}, u32[]{:S(2)}) async-start(bf16[16,33,8,128]{3,2,1,0:T(8,128)(2,1)} %cut_tiles.1), calls=%async_computation | async-start | bytes 2162688 | tf_op jit(solution)/shard_map/all_to_all | solution.py:245
  11.4 20.9 %copy-start.8 = (bf16[256,160]{1,0:T(8,128)(2,1)S(1)}, bf16[256,160]{1,0:T(8,128)(2,1)}, u32[]{:S(2)}) copy-start(bf16[256,160]{1,0:T(8,128)(2,1)} %get-tuple-element.7) | copy-start | bytes 245764
  25.8 20.4 %all-to-all-start.1 = ((bf16[16,13,8,128]{3,2,1,0:T(8,128)(2,1)}), bf16[16,13,8,128]{3,2,1,0:T(8,128)(2,1)S(1)}, u32[]{:S(2)}, u32[]{:S(2)}) async-start(bf16[16,13,8,128]{3,2,1,0:T(8,128)(2,1)} %broadcast_in_dim.3), calls=%async_computation.1 | async-start | bytes 851968 | tf_op jit(solution)/shard_map/all_to_all | solution.py:245
  32.3 6.6 %copy-start.6 = (bf16[1,160,7680]{2,1,0:T(8,128)(2,1)S(1)}, bf16[1,160,7680]{2,1,0:T(8,128)(2,1)}, u32[]{:S(2)}) copy-start(bf16[1,160,7680]{2,1,0:T(8,128)(2,1)} %param.8) | copy-start | bytes 7372804
  35.4 9.7 %copy-start = (bf16[1280,320]{0,1:T(8,128)(2,1)S(1)}, bf16[1280,320]{0,1:T(8,128)(2,1)}, u32[]{:S(2)}) copy-start(bf16[1280,320]{0,1:T(8,128)(2,1)} %param.12) | copy-start | bytes 2457604
  35.4 9.7 %copy-start.2 = (bf16[256,160]{1,0:T(8,128)(2,1)S(1)}, bf16[256,160]{1,0:T(8,128)(2,1)}, u32[]{:S(2)}) copy-start(bf16[256,160]{1,0:T(8,128)(2,1)} %get-tuple-element.8.table_ref) | copy-start | bytes 245764
  35.4 9.7 %copy-start.3 = (f32[1280]{0:T(1024)S(1)}, f32[1280]{0:T(1024)}, u32[]{:S(2)}) copy-start(f32[1280]{0:T(1024)} %gain_ref.1) | copy-start | bytes 15364
  35.4 9.7 %copy-start.4 = (f32[1280]{0:T(1024)S(1)}, f32[1280]{0:T(1024)}, u32[]{:S(2)}) copy-start(f32[1280]{0:T(1024)} %bias_ref.1) | copy-start | bytes 15364
  35.4 9.7 %copy-start.5 = (f32[320]{0:T(512)S(1)}, f32[320]{0:T(512)}, u32[]{:S(2)}) copy-start(f32[320]{0:T(512)} %fc1_bias_ref.1) | copy-start | bytes 3844
  35.4 28.6 %collective-permute-start = (bf16[64,6400]{1,0:T(8,128)(2,1)}, bf16[64,6400]{1,0:T(8,128)(2,1)}, u32[]{:S(2)}, u32[]{:S(2)}) collective-permute-start(bf16[64,6400]{1,0:T(8,128)(2,1)} %convolution_convert_fusion.2), channel_id=1, source_target_pairs={{0,4},{1,5},{2,6},{3,7},{4,8},{5,9},{6,10},{7,11},{8,12},{9,13},{1... | collective-permute-start | bytes 2457608 | tf_op jit(solution)/shard_map/ppermute | solution.py:274
  40.3 5.9 %copy-start.1 = (bf16[1280,320]{0,1:T(8,128)(2,1)S(1)}, bf16[1280,320]{0,1:T(8,128)(2,1)}, u32[]{:S(2)}) copy-start(bf16[1280,320]{0,1:T(8,128)(2,1)} %param.14) | copy-start | bytes 2457604
  40.3 23.7 %collective-permute-start.1 = (bf16[64,6400]{1,0:T(8,128)(2,1)}, bf16[64,6400]{1,0:T(8,128)(2,1)}, u32[]{:S(2)}, u32[]{:S(2)}) collective-permute-start(bf16[64,6400]{1,0:T(8,128)(2,1)} %convolution_convert_fusion.1), channel_id=1, source_target_pairs={{0,8},{1,9},{2,10},{3,11},{4,12},{5,13},{6,14},{7,15},{8,0},{9,1},... | collective-permute-start | bytes 2457608 | tf_op jit(solution)/shard_map/ppermute | solution.py:274
  46.2 4.9 %copy-start.9 = (bf16[256,160]{1,0:T(8,128)(2,1)S(1)}, bf16[256,160]{1,0:T(8,128)(2,1)}, u32[]{:S(2)}) copy-start(bf16[256,160]{1,0:T(8,128)(2,1)} %get-tuple-element.7) | copy-start | bytes 245764
  49.1 7.5 %copy-start.7 = (bf16[1,160,7680]{2,1,0:T(8,128)(2,1)S(1)}, bf16[1,160,7680]{2,1,0:T(8,128)(2,1)}, u32[]{:S(2)}) copy-start(bf16[1,160,7680]{2,1,0:T(8,128)(2,1)} %param.8) | copy-start | bytes 7372804
  49.1 7.9 %collective-permute-start.6 = (bf16[4,4,40,640]{3,2,1,0:T(8,128)(2,1)S(1)}, bf16[4,4,40,640]{3,2,1,0:T(8,128)(2,1)S(1)}, u32[]{:S(2)}, u32[]{:S(2)}) collective-permute-start(bf16[4,4,40,640]{3,2,1,0:T(8,128)(2,1)S(1)} %get-tuple-element.10), channel_id=1, source_target_pairs={{0,16},{16,0},{32,48},{48,32},{64,80},{80,64},{96,112},{112,96},{1... | collective-permute-start | bytes 2457608 | tf_op jit(solution)/shard_map/ppermute | solution.py:335
  53.1 14.2 %collective-permute-start.2 = (bf16[64,6400]{1,0:T(8,128)(2,1)S(1)}, bf16[64,6400]{1,0:T(8,128)(2,1)S(1)}, u32[]{:S(2)}, u32[]{:S(2)}) collective-permute-start(bf16[64,6400]{1,0:T(8,128)(2,1)S(1)} %convolution_convert_fusion), channel_id=1, source_target_pairs={{0,12},{1,13},{2,14},{3,15},{4,0},{5,1},{6,2},{7,3},{8,4},{9,5},{1... | collective-permute-start | bytes 2457608 | tf_op jit(solution)/shard_map/ppermute | solution.py:274
  58.1 23.2 %all-to-all-start.2 = ((bf16[4,4,40,640]{3,2,1,0:T(8,128)(2,1)}), bf16[4,4,40,640]{3,2,1,0:T(8,128)(2,1)S(1)}, u32[]{:S(2)}, u32[]{:S(2)}) async-start(bf16[4,4,40,640]{3,2,1,0:T(8,128)(2,1)} %add_convert_fusion), calls=%async_computation.2 | async-start | bytes 1638400 | tf_op jit(solution)/shard_map/all_to_all | solution.py:245
  69.2 23.7 %collective-permute-start.3 = (bf16[16,6400]{1,0:T(8,128)(2,1)S(1)}, bf16[16,6400]{1,0:T(8,128)(2,1)S(1)}, u32[]{:S(2)}, u32[]{:S(2)}) collective-permute-start(bf16[16,6400]{1,0:T(8,128)(2,1)S(1)} %get-tuple-element.14), channel_id=1, source_target_pairs={{0,1},{1,2},{2,3},{3,0},{4,5},{5,6},{6,7},{7,4},{8,9},{9,10},{10,1... | collective-permute-start | bytes 614408 | tf_op jit(solution)/shard_map/ppermute | solution.py:274
  71.7 21.3 %collective-permute-start.4 = (bf16[16,6400]{1,0:T(8,128)(2,1)S(1)}, bf16[16,6400]{1,0:T(8,128)(2,1)S(1)}, u32[]{:S(2)}, u32[]{:S(2)}) collective-permute-start(bf16[16,6400]{1,0:T(8,128)(2,1)S(1)} %get-tuple-element.13), channel_id=1, source_target_pairs={{0,2},{1,3},{2,0},{3,1},{4,6},{5,7},{6,4},{7,5},{8,10},{9,11},{10,... | collective-permute-start | bytes 614408 | tf_op jit(solution)/shard_map/ppermute | solution.py:274
  76.0 17.0 %collective-permute-start.5 = (bf16[16,6400]{1,0:T(8,128)(2,1)S(1)}, bf16[16,6400]{1,0:T(8,128)(2,1)S(1)}, u32[]{:S(2)}, u32[]{:S(2)}) collective-permute-start(bf16[16,6400]{1,0:T(8,128)(2,1)S(1)} %get-tuple-element.12), channel_id=1, source_target_pairs={{0,3},{1,0},{2,1},{3,2},{4,7},{5,4},{6,5},{7,6},{8,11},{9,8},{10,9... | collective-permute-start | bytes 614408 | tf_op jit(solution)/shard_map/ppermute | solution.py:274
  82.1 30.2 %all-to-all-start.3 = ((bf16[4,40,640]{2,1,0:T(8,128)(2,1)}), bf16[4,40,640]{2,1,0:T(8,128)(2,1)S(1)}, u32[]{:S(2)}, u32[]{:S(2)}) async-start(bf16[4,40,640]{2,1,0:T(8,128)(2,1)} %reduce_sum.37), calls=%async_computation.3 | async-start | bytes 409600 | tf_op jit(solution)/shard_map/all_to_all | solution.py:245

commit v3 on v2

--- a/solution.py
+++ b/solution.py
@@ -90,80 +90,69 @@
     return (preact * normal_cdf, normal_cdf + preact * density)
 
 
-def hidden_kernel(head, tiles_ref, gain_ref, bias_ref, weight_ref, fc1_bias_ref, table_ref, packed_ref):
+def hidden_kernel(head, tiles_ref, gain_ref, bias_ref, weight_ref, fc1_bias_ref, table_ref, later_ref, packed_ref):
     parts = tiles_ref.shape[0]
-    slots = packed_ref.shape[0]
+    slots = table_ref.shape[0]
     units, width = weight_ref.shape
     wide = -(-units // LANE) * LANE
     across = width // LANE
     per_part = slots // parts
+    later_at = packed_ref.shape[1] - width
+    packed_ref[:units, later_at:] = later_ref[...]
     for part in range(parts):
         for at in range(0, per_part, SUB):
             for c in range(across):
                 packed_ref[part * per_part + at : part * per_part + at + SUB, c * LANE : (c + 1) * LANE] = tiles_ref[
                     part, head + (at // SUB) * across + c
                 ]
-    values = packed_ref[:, :width].astype(jnp.float32)
+    values = packed_ref[:slots, :width].astype(jnp.float32)
     centered = values - jnp.mean(values, axis=1, keepdims=True)
     row_var = jnp.mean(centered * centered, axis=1, keepdims=True)
     normed = (centered / jnp.sqrt(row_var + 1e-05) * gain_ref[...][None] + bias_ref[...][None]).astype(jnp.bfloat16)
-    packed_ref[:, :width] = normed
+    packed_ref[:slots, :width] = normed
     preact = lax.dot_general(normed, weight_ref[...], (((1,), (1,)), ((), ())), preferred_element_type=jnp.float32)
     activated, derivative = gelu_parts(preact + fc1_bias_ref[...][None])
-    packed_ref[:, width:] = jnp.zeros((slots, packed_ref.shape[1] - width), jnp.bfloat16)
-    packed_ref[:, width + 2 * wide : width + 2 * wide + table_ref.shape[1]] = table_ref[...]
-    packed_ref[:, width + wide - units : width + wide] = activated.astype(jnp.bfloat16)
-    packed_ref[:, width + wide : width + wide + units] = derivative.astype(jnp.bfloat16)
-
-
-def hidden_parts(tiles, head, gain, bias, weight_t, fc1_bias, table):
+    packed_ref[:slots, width:later_at] = jnp.zeros((slots, later_at - width), jnp.bfloat16)
+    packed_ref[:slots, width + 2 * wide : width + 2 * wide + table_ref.shape[1]] = table_ref[...]
+    packed_ref[:slots, width + wide - units : width + wide] = activated.astype(jnp.bfloat16)
+    packed_ref[:slots, width + wide : width + wide + units] = derivative.astype(jnp.bfloat16)
+
+
+def hidden_parts(tiles, head, gain, bias, weight_t, fc1_bias, table, later):
     units, width = weight_t.shape
     slots = tiles.shape[0] * SLOT_PAD
     wide = -(-units // LANE) * LANE
     spare = -(-table.shape[1] // LANE) * LANE
     return pl.pallas_call(
         functools.partial(hidden_kernel, head),
-        out_shape=jax.ShapeDtypeStruct((slots, width + 2 * wide + spare), jnp.bfloat16),
+        out_shape=jax.ShapeDtypeStruct((max(slots, units), 2 * width + 2 * wide + spare), jnp.bfloat16),
         name="hidden_parts",
         compiler_params=pltpu.CompilerParams(vmem_limit_bytes=16 << 20),
-    )(tiles, gain, bias, weight_t, fc1_bias, table)
-
-
-def grads_kernel(places, factor, *refs):
-    sources, (mine_hbm, theirs_hbm), scratch = refs[:3], refs[3:5], refs[5:]
-    tiles_ref, packed_ref, weight_ref = scratch[:3]
-    mine_ref, theirs_ref, rows_ref, up_ref, pg_ref, in_sem, out_sem = scratch[3:]
-    width = up_ref.shape[1]
-    loads = [pltpu.make_async_copy(src, dst, in_sem.at[i]) for i, (src, dst) in enumerate(zip(sources, scratch[:3]))]
-    for load in loads:
-        load.start()
-    loads[0].wait()
+    )(tiles, gain, bias, weight_t, fc1_bias, table, later)
+
+
+def grads_kernel(places, factor, units, tiles_ref, packed_ref, mine_ref, theirs_ref, rows_ref, up_ref, pg_ref):
+    rows, width = rows_ref.shape
+    slots, wide = pg_ref.shape
+    later_at = packed_ref.shape[1] - width
     for part, i, at, size, r, c in places:
         rows_ref[r : r + size, c : c + LANE] = tiles_ref[part, i, at : at + size, :]
-    loads[1].wait()
-    table_at = width + 2 * pg_ref.shape[1]
-    table = packed_ref[:, table_at : table_at + rows_ref.shape[0]]
+    table = packed_ref[:slots, width + 2 * wide : width + 2 * wide + rows]
     up_ref[...] = jnp.dot(table, rows_ref[...], preferred_element_type=jnp.float32).astype(jnp.bfloat16)
-    loads[2].wait()
     hidden_grad = lax.dot_general(
-        up_ref[...], weight_ref[...], (((1,), (1,)), ((), ())), preferred_element_type=jnp.float32
+        up_ref[...], packed_ref[:units, later_at:], (((1,), (1,)), ((), ())), preferred_element_type=jnp.float32
     )
-    units = hidden_grad.shape[1]
-    deriv_at = width + pg_ref.shape[1]
+    deriv = packed_ref[:slots, width + wide : width + wide + units].astype(jnp.float32)
     pg_ref[...] = jnp.zeros_like(pg_ref)
-    pg_ref[:, :units] = (hidden_grad * packed_ref[:, deriv_at : deriv_at + units].astype(jnp.float32)).astype(jnp.bfloat16)
-    near, far, block, _ = mine_ref.shape
-    wide = pg_ref.shape[1]
+    pg_ref[:, :units] = (hidden_grad * deriv).astype(jnp.bfloat16)
+    near, _, block, _ = mine_ref.shape
     keep = wide - LANE
-    halves = 2
-    step = width // halves
+    step = width // 2
     low = lax.axis_index("dp") % 2 == 0
-    stores = []
-    for turn in range(halves):
-        at = turn * step
+    hidden = packed_ref[:slots, width : width + wide]
+    for at in range(0, width, step):
         dims = (((0,), (0,)), ((), ()))
-        first = lax.dot_general(packed_ref[:, at : at + step], pg_ref[...], dims, preferred_element_type=jnp.float32)
-        hidden = packed_ref[:, width : width + wide]
+        first = lax.dot_general(packed_ref[:slots, at : at + step], pg_ref[...], dims, preferred_element_type=jnp.float32)
         second = lax.dot_general(up_ref[:, at : at + step], hidden, dims, preferred_element_type=jnp.float32)
         for b in range(0, step, 2 * block):
             m, p = divmod((at + b) // (2 * block), near)
@@ -174,40 +163,23 @@
             for lo, hi, start in zip(*parts, (0, keep, wide)):
                 mine_ref[p, m, :, start : start + lo.shape[1]] = jnp.where(low, lo, hi).astype(jnp.bfloat16)
                 theirs_ref[p, m, :, start : start + lo.shape[1]] = jnp.where(low, hi, lo).astype(jnp.bfloat16)
-        some = pl.ds(turn * (far // halves), far // halves)
-        for j, (src, dst) in enumerate(((theirs_ref, theirs_hbm), (mine_ref, mine_hbm))):
-            store = pltpu.make_async_copy(src.at[:, some], dst.at[:, some], out_sem.at[2 * turn + j])
-            store.start()
-            stores.append(store)
-    for store in stores:
-        store.wait()
-
-
-def grad_terms(tiles, packed, weight_t, rows, factor, shape):
-    units, width = weight_t.shape
-    slots = packed.shape[0]
+
+
+def grad_terms(tiles, packed, units, width, rows, factor, shape):
+    slots = tiles.shape[0] * SLOT_PAD
     wide = -(-units // LANE) * LANE
     _, places = tile_places(rows, width, tiles.shape[0])
-    operands = (tiles, packed, weight_t)
-    anywhere = pl.BlockSpec(memory_space=pl.ANY)
     return pl.pallas_call(
-        functools.partial(grads_kernel, places, factor),
-        in_specs=[anywhere] * len(operands),
-        out_specs=(anywhere,) * 2,
+        functools.partial(grads_kernel, places, factor, units),
         out_shape=(jax.ShapeDtypeStruct(shape, jnp.bfloat16),) * 2,
-        scratch_shapes=[pltpu.VMEM(a.shape, a.dtype) for a in operands]
-        + [
-            pltpu.VMEM(shape, jnp.bfloat16),
-            pltpu.VMEM(shape, jnp.bfloat16),
+        scratch_shapes=[
             pltpu.VMEM((rows, width), jnp.bfloat16),
             pltpu.VMEM((slots, width), jnp.bfloat16),
             pltpu.VMEM((slots, wide), jnp.bfloat16),
-            pltpu.SemaphoreType.DMA((len(operands),)),
-            pltpu.SemaphoreType.DMA((4,)),
         ],
         name="grad_terms",
         compiler_params=pltpu.CompilerParams(vmem_limit_bytes=GRADS_VMEM << 20),
-    )(*operands)
+    )(tiles, packed)
 
 
 def tables_kernel(side, ranks_ref, table_ref, early_ref):
@@ -324,12 +296,12 @@
     tiles = to_all(own_tiles, "tp")
 
     table, early_table = slot_tables(row_rank.T, groups)
-    packed = hidden_parts(arrived, head, ln_gain, ln_bias, fc1_weight.T, fc1_bias, table)
+    packed = hidden_parts(arrived, head, ln_gain, ln_bias, fc1_weight.T, fc1_bias, table, fc2_weight.T)
     placed = route_early(local_part[:, width:], early_table, replicas, groups)[:slot_count]
 
     factor = float(replicas * row_count) ** (-0.5)
     mine, theirs = grad_terms(
-        tiles, packed, fc2_weight.T, row_count, factor,
+        tiles, packed, units, width, row_count, factor,
         (near, far, block, 2 * units),
     )
     theirs = lax.ppermute(theirs, "dp", pairs)

time: 114 us -> 113 us (level)
  the two profiles are of different devices: /device:TPU:56 before, /device:TPU:58 now
where the time goes in v3:
time: 113 us; the launch traced here: 112 us
  starting transfers between devices  56.6 us (50%)
  waiting for transfers between devices  35.5 us (31%)
  Pallas kernels  7.37 us (7%)
  matrix products  5.09 us (5%)
  other arithmetic  4.61 us (4%)
  local copies, waits for them, and re-layouts  1.61 us (1%)
    all_to_all x4, starting transfers between devices, exchange(): lax.all_to_all(blocks, axis, 0, 0, tiled=True, axis_index_groups=groups)  34.3 us
    all_to_all x4, waiting for transfers between devices, exchange(): lax.all_to_all(blocks, axis, 0, 0, tiled=True, axis_index_groups=groups)  31.7 us
    ppermute x6, starting transfers between devices, named_permute(): return lax.ppermute(value, ('dp', 'tp'), pairs)  20.4 us
    dot_general x4, matrix products, route_early(): jnp.dot(table[d * span:(d + 1) * span], part, preferred_element_type=jnp....  5.09 us
    ppermute x6, waiting for transfers between devices, named_permute(): return lax.ppermute(value, ('dp', 'tp'), pairs)  3.79 us
    convert_element_type x3, other arithmetic, summed(): sum((b.astype(jnp.float32) for b in moved), own.astype(jnp.float32))  3.69 us
    pallas_call x1, Pallas kernels, grad_terms(): pl.pallas_call(functools.partial(grads_kernel, places, factor, units), ou...  2.69 us
  transfers between devices with their start and end apart: 11, of which 4 were waited for; matrix products, arithmetic and copies ran while one was open for 9% of the time, Pallas kernels for 5%

profile of v3, /device:TPU:58, one launch (start us, length us, event | category | flops | bytes accessed | tf_op | source)
XLA Modules:
  0.0 111.6 jit_solution(7682781914711081202)
XLA Ops:
  0.6 2.0 %cut_tiles.1 = bf16[16,33,8,128]{3,2,1,0:T(8,128)(2,1)} custom-call(bf16[160,7680]{1,0:T(8,128)(2,1)} %bitcast.6, bf16[15,1280]{1,0:T(8,128)(2,1)} %layer_hbm.1), custom_call_target="tpu_custom_call" | custom-call | tf_op jit(solution)/shard_map/cut_tiles/pallas_call | solution.py:71
  2.6 7.3 %all-to-all-start = ((bf16[16,33,8,128]{3,2,1,0:T(8,128)(2,1)}), bf16[16,33,8,128]{3,2,1,0:T(8,128)(2,1)S(1)}, u32[]{:S(2)}, u32[]{:S(2)}) async-start(bf16[16,33,8,128]{3,2,1,0:T(8,128)(2,1)} %cut_tiles.1), calls=%async_computation | async-start | bytes 2162688 | tf_op jit(solution)/shard_map/all_to_all | solution.py:217
  9.9 1.6 %slot_tables.1 = (bf16[256,160]{1,0:T(8,128)(2,1)}, bf16[256,160]{1,0:T(8,128)(2,1)}) custom-call(s32[1,160]{1,0:T(1,128)} %bitcast.11), custom_call_target="tpu_custom_call" | custom-call | tf_op jit(solution)/shard_map/slot_tables/pallas_call | solution.py:211
  11.5 12.6 %all-to-all-done.tiles_ref = bf16[16,33,8,128]{3,2,1,0:T(8,128)(2,1)S(1)} async-done(((bf16[16,33,8,128]{3,2,1,0:T(8,128)(2,1)}), bf16[16,33,8,128]{3,2,1,0:T(8,128)(2,1)S(1)}, u32[]{:S(2)}, u32[]{:S(2)}) %all-to-all-start) | async-done | bytes 1081376 | tf_op jit(solution)/shard_map/all_to_all | solution.py:217
  24.1 0.1 slice_reduce_fusion
  24.1 0.8 broadcast_in_dim.3
  24.9 8.1 %all-to-all-start.1 = ((bf16[16,13,8,128]{3,2,1,0:T(8,128)(2,1)}), bf16[16,13,8,128]{3,2,1,0:T(8,128)(2,1)}, u32[]{:S(2)}, u32[]{:S(2)}) async-start(bf16[16,13,8,128]{3,2,1,0:T(8,128)(2,1)} %broadcast_in_dim.3), calls=%async_computation.1 | async-start | bytes 851968 | tf_op jit(solution)/shard_map/all_to_all | solution.py:217
  33.0 2.1 %convolution_convert_fusion.2 = bf16[64,6400]{1,0:T(8,128)(2,1)} fusion(bf16[160,7680]{1,0:T(8,128)(2,1)S(1)} %bitcast.7, bf16[256,160]{1,0:T(8,128)(2,1)} %get-tuple-element.7), kind=kOutput, calls=%fused_computation.2 | convolution fusion | flops 131481600 | bytes 2899968 | tf_op jit(solution)/shard_map/dot_general | solution.py:259
  35.1 0.0 copy-start.5
  35.2 3.6 %collective-permute-start = (bf16[64,6400]{1,0:T(8,128)(2,1)}, bf16[64,6400]{1,0:T(8,128)(2,1)}, u32[]{:S(2)}, u32[]{:S(2)}) collective-permute-start(bf16[64,6400]{1,0:T(8,128)(2,1)} %convolution_convert_fusion.2), channel_id=1, source_target_pairs={{0,4},{1,5},{2,6},{3,7},{4,8},{5,9},{6,10},{7,11},{8,12},{9,13},{1... | collective-permute-start | bytes 2457608 | tf_op jit(solution)/shard_map/ppermute | solution.py:246
  38.7 2.1 %convolution_convert_fusion.1 = bf16[64,6400]{1,0:T(8,128)(2,1)} fusion(bf16[160,7680]{1,0:T(8,128)(2,1)S(1)} %bitcast.8, bf16[256,160]{1,0:T(8,128)(2,1)} %get-tuple-element.7), kind=kOutput, calls=%fused_computation.1 | convolution fusion | flops 131481600 | bytes 2899968 | tf_op jit(solution)/shard_map/dot_general | solution.py:259
  40.9 3.0 %collective-permute-start.1 = (bf16[64,6400]{1,0:T(8,128)(2,1)}, bf16[64,6400]{1,0:T(8,128)(2,1)}, u32[]{:S(2)}, u32[]{:S(2)}) collective-permute-start(bf16[64,6400]{1,0:T(8,128)(2,1)} %convolution_convert_fusion.1), channel_id=1, source_target_pairs={{0,8},{1,9},{2,10},{3,11},{4,12},{5,13},{6,14},{7,15},{8,0},{9,1},... | collective-permute-start | bytes 2457608 | tf_op jit(solution)/shard_map/ppermute | solution.py:246
  43.9 1.1 hidden_parts.1.packed_ref
  45.1 2.7 %grad_terms.1 = (bf16[4,4,40,640]{3,2,1,0:T(8,128)(2,1)S(1)}, bf16[4,4,40,640]{3,2,1,0:T(8,128)(2,1)S(1)}) custom-call(bf16[16,13,8,128]{3,2,1,0:T(8,128)(2,1)} %all-to-all-done.1.tiles_ref, bf16[320,3584]{1,0:T(8,128)(2,1)S(1)} %hidden_parts.1.packed_ref), custom_call_target="tpu_custom_call" | custom-call | tf_op jit(solution)/shard_map/grad_terms/pallas_call | solution.py:172
  47.8 1.9 %collective-permute-start.6 = (bf16[4,4,40,640]{3,2,1,0:T(8,128)(2,1)S(1)}, bf16[4,4,40,640]{3,2,1,0:T(8,128)(2,1)S(1)}, u32[]{:S(2)}, u32[]{:S(2)}) collective-permute-start(bf16[4,4,40,640]{3,2,1,0:T(8,128)(2,1)S(1)} %get-tuple-element.10), channel_id=1, source_target_pairs={{0,16},{16,0},{32,48},{48,32},{64,80},{80,64},{96,112},{112,96},{1... | collective-permute-start | bytes 2457608 | tf_op jit(solution)/shard_map/ppermute | solution.py:307
  49.7 0.5 convolution_convert_fusion
  50.2 4.1 %collective-permute-start.2 = (bf16[64,6400]{1,0:T(8,128)(2,1)S(1)}, bf16[64,6400]{1,0:T(8,128)(2,1)S(1)}, u32[]{:S(2)}, u32[]{:S(2)}) collective-permute-start(bf16[64,6400]{1,0:T(8,128)(2,1)S(1)} %convolution_convert_fusion), channel_id=1, source_target_pairs={{0,12},{1,13},{2,14},{3,15},{4,0},{5,1},{6,2},{7,3},{8,4},{9,5},{1... | collective-permute-start | bytes 2457608 | tf_op jit(solution)/shard_map/ppermute | solution.py:246
  54.2 0.4 convolution_convert_fusion.3
  54.7 1.1 add_convert_fusion
  55.8 6.0 %all-to-all-start.2 = ((bf16[4,4,40,640]{3,2,1,0:T(8,128)(2,1)}), bf16[4,4,40,640]{3,2,1,0:T(8,128)(2,1)S(1)}, u32[]{:S(2)}, u32[]{:S(2)}) async-start(bf16[4,4,40,640]{3,2,1,0:T(8,128)(2,1)} %add_convert_fusion), calls=%async_computation.2 | async-start | bytes 1638400 | tf_op jit(solution)/shard_map/all_to_all | solution.py:217
  61.8 3.8 %collective-permute-done.2 = bf16[64,6400]{1,0:T(8,128)(2,1)S(1)} collective-permute-done((bf16[64,6400]{1,0:T(8,128)(2,1)S(1)}, bf16[64,6400]{1,0:T(8,128)(2,1)S(1)}, u32[]{:S(2)}, u32[]{:S(2)}) %collective-permute-start.2) | collective-permute-done | bytes 819232 | tf_op jit(solution)/shard_map/ppermute | solution.py:246
  65.6 1.8 %add_convert_fusion.1 = bf16[64,6400]{1,0:T(8,128)(2,1)S(1)} fusion(bf16[64,6400]{1,0:T(8,128)(2,1)S(1)} %collective-permute-done.2, bf16[64,6400]{1,0:T(8,128)(2,1)} %collective-permute-done.1, bf16[64,6400]{1,0:T(8,128)(2,1)} %collective-permute-done, bf16[64,6400]{1,0:T(8,128)(2,1)S(1)} %convolution_convert_fusion.3), kind=kLoop, calls=%fused_computation.5 | loop fusion | flops 3276800 | bytes 4096000 | tf_op jit(solution)/shard_map/convert_element_type | solution.py:250
  67.4 0.1 fusion.8
  67.4 2.7 %collective-permute-start.5 = (bf16[16,6400]{1,0:T(8,128)(2,1)S(1)}, bf16[16,6400]{1,0:T(8,128)(2,1)S(1)}, u32[]{:S(2)}, u32[]{:S(2)}) collective-permute-start(bf16[16,6400]{1,0:T(8,128)(2,1)S(1)} %get-tuple-element.12), channel_id=1, source_target_pairs={{0,3},{1,0},{2,1},{3,2},{4,7},{5,4},{6,5},{7,6},{8,11},{9,8},{10,9... | collective-permute-start | bytes 614408 | tf_op jit(solution)/shard_map/ppermute | solution.py:246
  70.1 3.1 %collective-permute-start.4 = (bf16[16,6400]{1,0:T(8,128)(2,1)S(1)}, bf16[16,6400]{1,0:T(8,128)(2,1)S(1)}, u32[]{:S(2)}, u32[]{:S(2)}) collective-permute-start(bf16[16,6400]{1,0:T(8,128)(2,1)S(1)} %get-tuple-element.13), channel_id=1, source_target_pairs={{0,2},{1,3},{2,0},{3,1},{4,6},{5,7},{6,4},{7,5},{8,10},{9,11},{10,... | collective-permute-start | bytes 614408 | tf_op jit(solution)/shard_map/ppermute | solution.py:246
  73.2 4.0 %collective-permute-start.3 = (bf16[16,6400]{1,0:T(8,128)(2,1)S(1)}, bf16[16,6400]{1,0:T(8,128)(2,1)S(1)}, u32[]{:S(2)}, u32[]{:S(2)}) collective-permute-start(bf16[16,6400]{1,0:T(8,128)(2,1)S(1)} %get-tuple-element.14), channel_id=1, source_target_pairs={{0,1},{1,2},{2,3},{3,0},{4,5},{5,6},{6,7},{7,4},{8,9},{9,10},{10,1... | collective-permute-start | bytes 614408 | tf_op jit(solution)/shard_map/ppermute | solution.py:246
  77.2 1.3 %all-to-all-done.2 = bf16[4,4,40,640]{3,2,1,0:T(8,128)(2,1)S(1)} async-done(((bf16[4,4,40,640]{3,2,1,0:T(8,128)(2,1)}), bf16[4,4,40,640]{3,2,1,0:T(8,128)(2,1)S(1)}, u32[]{:S(2)}, u32[]{:S(2)}) %all-to-all-start.2) | async-done | bytes 819232 | tf_op jit(solution)/shard_map/all_to_all | solution.py:217
  78.5 0.8 reduce_sum.37
  79.3 12.9 %all-to-all-start.3 = ((bf16[4,40,640]{2,1,0:T(8,128)(2,1)}), bf16[4,40,640]{2,1,0:T(8,128)(2,1)S(1)}, u32[]{:S(2)}, u32[]{:S(2)}) async-start(bf16[4,40,640]{2,1,0:T(8,128)(2,1)} %reduce_sum.37), calls=%async_computation.3 | async-start | bytes 409600 | tf_op jit(solution)/shard_map/all_to_all | solution.py:217
  92.3 0.8 add_convert_fusion.2
  93.1 17.9 %all-to-all-done.3 = bf16[4,40,640]{2,1,0:T(8,128)(2,1)S(1)} async-done(((bf16[4,40,640]{2,1,0:T(8,128)(2,1)}), bf16[4,40,640]{2,1,0:T(8,128)(2,1)S(1)}, u32[]{:S(2)}, u32[]{:S(2)}) %all-to-all-start.3) | async-done | bytes 204832 | tf_op jit(solution)/shard_map/all_to_all | solution.py:217
  111.0 0.7 fusion.9
  (25 shorter events, 0.1 us)
Async XLA Ops:
  2.6 30.4 %copy-start.6 = (bf16[1,160,7680]{2,1,0:T(8,128)(2,1)S(1)}, bf16[1,160,7680]{2,1,0:T(8,128)(2,1)}, u32[]{:S(2)}) copy-start(bf16[1,160,7680]{2,1,0:T(8,128)(2,1)} %param.8) | copy-start | bytes 7372804
  2.6 21.4 %all-to-all-start = ((bf16[16,33,8,128]{3,2,1,0:T(8,128)(2,1)}), bf16[16,33,8,128]{3,2,1,0:T(8,128)(2,1)S(1)}, u32[]{:S(2)}, u32[]{:S(2)}) async-start(bf16[16,33,8,128]{3,2,1,0:T(8,128)(2,1)} %cut_tiles.1), calls=%async_computation | async-start | bytes 2162688 | tf_op jit(solution)/shard_map/all_to_all | solution.py:217
  24.9 20.1 %all-to-all-start.1 = ((bf16[16,13,8,128]{3,2,1,0:T(8,128)(2,1)}), bf16[16,13,8,128]{3,2,1,0:T(8,128)(2,1)}, u32[]{:S(2)}, u32[]{:S(2)}) async-start(bf16[16,13,8,128]{3,2,1,0:T(8,128)(2,1)} %broadcast_in_dim.3), calls=%async_computation.1 | async-start | bytes 851968 | tf_op jit(solution)/shard_map/all_to_all | solution.py:217
  35.1 8.7 %copy-start = (bf16[1280,320]{0,1:T(8,128)(2,1)S(1)}, bf16[1280,320]{0,1:T(8,128)(2,1)}, u32[]{:S(2)}) copy-start(bf16[1280,320]{0,1:T(8,128)(2,1)} %param.12) | copy-start | bytes 2457604
  35.1 8.7 %copy-start.1 = (bf16[1280,320]{0,1:T(8,128)(2,1)S(1)}, bf16[1280,320]{0,1:T(8,128)(2,1)}, u32[]{:S(2)}) copy-start(bf16[1280,320]{0,1:T(8,128)(2,1)} %param.14) | copy-start | bytes 2457604
  35.1 8.7 %copy-start.2 = (bf16[256,160]{1,0:T(8,128)(2,1)S(1)}, bf16[256,160]{1,0:T(8,128)(2,1)}, u32[]{:S(2)}) copy-start(bf16[256,160]{1,0:T(8,128)(2,1)} %get-tuple-element.8.table_ref) | copy-start | bytes 245764
  35.1 8.8 %copy-start.3 = (f32[1280]{0:T(1024)S(1)}, f32[1280]{0:T(1024)}, u32[]{:S(2)}) copy-start(f32[1280]{0:T(1024)} %gain_ref.1) | copy-start | bytes 15364
  35.1 8.8 %copy-start.4 = (f32[1280]{0:T(1024)S(1)}, f32[1280]{0:T(1024)}, u32[]{:S(2)}) copy-start(f32[1280]{0:T(1024)} %bias_ref.1) | copy-start | bytes 15364
  35.1 8.8 %copy-start.5 = (f32[320]{0:T(512)S(1)}, f32[320]{0:T(512)}, u32[]{:S(2)}) copy-start(f32[320]{0:T(512)} %fc1_bias_ref.1) | copy-start | bytes 3844
  35.2 26.6 %collective-permute-start = (bf16[64,6400]{1,0:T(8,128)(2,1)}, bf16[64,6400]{1,0:T(8,128)(2,1)}, u32[]{:S(2)}, u32[]{:S(2)}) collective-permute-start(bf16[64,6400]{1,0:T(8,128)(2,1)} %convolution_convert_fusion.2), channel_id=1, source_target_pairs={{0,4},{1,5},{2,6},{3,7},{4,8},{5,9},{6,10},{7,11},{8,12},{9,13},{1... | collective-permute-start | bytes 2457608 | tf_op jit(solution)/shard_map/ppermute | solution.py:246
  40.9 20.9 %collective-permute-start.1 = (bf16[64,6400]{1,0:T(8,128)(2,1)}, bf16[64,6400]{1,0:T(8,128)(2,1)}, u32[]{:S(2)}, u32[]{:S(2)}) collective-permute-start(bf16[64,6400]{1,0:T(8,128)(2,1)} %convolution_convert_fusion.1), channel_id=1, source_target_pairs={{0,8},{1,9},{2,10},{3,11},{4,12},{5,13},{6,14},{7,15},{8,0},{9,1},... | collective-permute-start | bytes 2457608 | tf_op jit(solution)/shard_map/ppermute | solution.py:246
  45.0 4.7 %copy-start.8 = (bf16[256,160]{1,0:T(8,128)(2,1)S(1)}, bf16[256,160]{1,0:T(8,128)(2,1)}, u32[]{:S(2)}) copy-start(bf16[256,160]{1,0:T(8,128)(2,1)} %get-tuple-element.7) | copy-start | bytes 245764
  45.1 4.7 %copy-start.7 = (bf16[1,160,7680]{2,1,0:T(8,128)(2,1)S(1)}, bf16[1,160,7680]{2,1,0:T(8,128)(2,1)}, u32[]{:S(2)}) copy-start(bf16[1,160,7680]{2,1,0:T(8,128)(2,1)} %param.8) | copy-start | bytes 7372804
  47.8 6.9 %collective-permute-start.6 = (bf16[4,4,40,640]{3,2,1,0:T(8,128)(2,1)S(1)}, bf16[4,4,40,640]{3,2,1,0:T(8,128)(2,1)S(1)}, u32[]{:S(2)}, u32[]{:S(2)}) collective-permute-start(bf16[4,4,40,640]{3,2,1,0:T(8,128)(2,1)S(1)} %get-tuple-element.10), channel_id=1, source_target_pairs={{0,16},{16,0},{32,48},{48,32},{64,80},{80,64},{96,112},{112,96},{1... | collective-permute-start | bytes 2457608 | tf_op jit(solution)/shard_map/ppermute | solution.py:307
  50.2 15.4 %collective-permute-start.2 = (bf16[64,6400]{1,0:T(8,128)(2,1)S(1)}, bf16[64,6400]{1,0:T(8,128)(2,1)S(1)}, u32[]{:S(2)}, u32[]{:S(2)}) collective-permute-start(bf16[64,6400]{1,0:T(8,128)(2,1)S(1)} %convolution_convert_fusion), channel_id=1, source_target_pairs={{0,12},{1,13},{2,14},{3,15},{4,0},{5,1},{6,2},{7,3},{8,4},{9,5},{1... | collective-permute-start | bytes 2457608 | tf_op jit(solution)/shard_map/ppermute | solution.py:246
  55.8 22.7 %all-to-all-start.2 = ((bf16[4,4,40,640]{3,2,1,0:T(8,128)(2,1)}), bf16[4,4,40,640]{3,2,1,0:T(8,128)(2,1)S(1)}, u32[]{:S(2)}, u32[]{:S(2)}) async-start(bf16[4,4,40,640]{3,2,1,0:T(8,128)(2,1)} %add_convert_fusion), calls=%async_computation.2 | async-start | bytes 1638400 | tf_op jit(solution)/shard_map/all_to_all | solution.py:217
  67.4 24.8 %collective-permute-start.5 = (bf16[16,6400]{1,0:T(8,128)(2,1)S(1)}, bf16[16,6400]{1,0:T(8,128)(2,1)S(1)}, u32[]{:S(2)}, u32[]{:S(2)}) collective-permute-start(bf16[16,6400]{1,0:T(8,128)(2,1)S(1)} %get-tuple-element.12), channel_id=1, source_target_pairs={{0,3},{1,0},{2,1},{3,2},{4,7},{5,4},{6,5},{7,6},{8,11},{9,8},{10,9... | collective-permute-start | bytes 614408 | tf_op jit(solution)/shard_map/ppermute | solution.py:246
  70.1 22.1 %collective-permute-start.4 = (bf16[16,6400]{1,0:T(8,128)(2,1)S(1)}, bf16[16,6400]{1,0:T(8,128)(2,1)S(1)}, u32[]{:S(2)}, u32[]{:S(2)}) collective-permute-start(bf16[16,6400]{1,0:T(8,128)(2,1)S(1)} %get-tuple-element.13), channel_id=1, source_target_pairs={{0,2},{1,3},{2,0},{3,1},{4,6},{5,7},{6,4},{7,5},{8,10},{9,11},{10,... | collective-permute-start | bytes 614408 | tf_op jit(solution)/shard_map/ppermute | solution.py:246
  73.2 19.0 %collective-permute-start.3 = (bf16[16,6400]{1,0:T(8,128)(2,1)S(1)}, bf16[16,6400]{1,0:T(8,128)(2,1)S(1)}, u32[]{:S(2)}, u32[]{:S(2)}) collective-permute-start(bf16[16,6400]{1,0:T(8,128)(2,1)S(1)} %get-tuple-element.14), channel_id=1, source_target_pairs={{0,1},{1,2},{2,3},{3,0},{4,5},{5,6},{6,7},{7,4},{8,9},{9,10},{10,1... | collective-permute-start | bytes 614408 | tf_op jit(solution)/shard_map/ppermute | solution.py:246
  79.3 31.6 %all-to-all-start.3 = ((bf16[4,40,640]{2,1,0:T(8,128)(2,1)}), bf16[4,40,640]{2,1,0:T(8,128)(2,1)S(1)}, u32[]{:S(2)}, u32[]{:S(2)}) async-start(bf16[4,40,640]{2,1,0:T(8,128)(2,1)} %reduce_sum.37), calls=%async_computation.3 | async-start | bytes 409600 | tf_op jit(solution)/shard_map/all_to_all | solution.py:217
